TPU v7x, 32 devices: a whole 2x2x4 slice. The times are simulated.
32 devices in a mesh: seq: 8 (over z, y), head: 4 (over x, core).
Axes of the slice: x: 2, y: 2, z: 4, core: 2. Of those that a mesh axis runs over, the one named last changes fastest.
Arguments:
- hidden: bfloat16 [4096, 8192], P('seq', 'head'), may hold values from -6 to 6
- gain: float32 [8192], replicated, may hold values from 0.25 to 1.75
- key_matrix: bfloat16 [8192, 512], P(None, 'head'), may hold values from -0.0625 to 0.0625
- value_matrix: bfloat16 [8192, 512], P(None, 'head'), may hold values from -0.0625 to 0.0625
- queries: bfloat16 [64, 4096], P(None, 'head'), may hold values from -360 to 360
- window_len: int32 [4], P('head'), may hold values from 16 to 64, as said below
- kernel_width: int32 [4], P('head'), may hold values from 1 to 15, as said below
- kept_block_count: int32 [4], P('head'), may hold values from 1 to 16
Outputs:
- block_scores: float32 [4, 32], P('head', 'seq')
- kept_fraction: float32 [4], P('head')
Inputs may be any that keep to these rules, and one draw needn't show every extreme that they name: `window_len`: at least one key-value head uses all 64 window queries. `kernel_width`: odd; at least one key-value head has width 15.
All inputs are finite; a program needn't handle non-finite values.
Results may differ from a plain program's by a relative error of at most 0.0112.
The roundings to bfloat16 on the way count: a program that leaves them out, or rounds other values in their place, can miss the bound.
Values may be sent and summed in bfloat16 or wider, within the bound.
No kernel may reach another device: no remote copies, remote signals or barrier semaphores. Data moves between devices by JAX's collectives and lax.ppermute only.
A program may use at most 128 MiB of HBM per device.

v0:
```python
import functools

import jax
import jax.numpy as jnp
from jax import lax
from jax.experimental import pallas as pl
from jax.experimental.pallas import tpu as pltpu
from jax.sharding import PartitionSpec as P

BLK = 128
LANES = 128
KERNEL_LIMIT = 15
REACH = (KERNEL_LIMIT - 1) // 2
EDGE = 16
CORES = 2
GROUP = 4
MASKED = -1e30

VMEM = pl.BlockSpec(memory_space=pltpu.VMEM)
SMEM = pl.BlockSpec(memory_space=pltpu.SMEM)
F32, BF16 = jnp.float32, jnp.bfloat16


def sds(shape, dtype):
    return jax.ShapeDtypeStruct(shape, dtype)


def call(body, out, ins, scratch=(), outs=None, flops=1 << 20, limit=40 << 20):
    return pl.pallas_call(
        body,
        out_shape=out,
        in_specs=ins,
        out_specs=outs if outs is not None else jax.tree.map(lambda _: VMEM, out),
        scratch_shapes=list(scratch),
        cost_estimate=pl.CostEstimate(flops=flops, bytes_accessed=1 << 20, transcendentals=0),
        compiler_params=pltpu.CompilerParams(vmem_limit_bytes=limit),
    )


def iota(shape, dim):
    return lax.broadcasted_iota(jnp.int32, shape, dim)


def to_lanes(col):
    n = col.shape[0]
    here = iota((n, LANES), 0) == iota((n, LANES), 1)
    return jnp.sum(jnp.where(here, jnp.broadcast_to(col, (n, LANES)), 0.0), axis=0, keepdims=True)


def to_rows(row, n):
    here = iota((n, LANES), 0) == iota((n, LANES), 1)
    return jnp.sum(jnp.where(here, jnp.broadcast_to(row, (n, LANES)), 0.0), axis=1, keepdims=True)


def norm_kernel(at, hid, gain, weights, *refs):
    more = refs[:-3]
    normed, sumsq, acc = refs[-3:]
    tok, feats = hid.shape
    q = feats // GROUP
    line = at[0]
    sumsq[...] = more[0][...] if more else jnp.zeros_like(sumsq)
    for b in range(tok // LANES):
        rows = pl.ds(b * LANES, LANES)
        folded = None
        for j in range(GROUP):
            place = (at[1] ^ j) * q
            for t in range(q // LANES):
                raw = hid[rows, pl.ds(j * q + t * LANES, LANES)].astype(F32)
                folded = raw * raw if folded is None else folded + raw * raw
                lanes = pl.ds(pl.multiple_of(place + t * LANES, LANES), LANES)
                scale = gain[pl.ds(line + j * (q // LANES) + t, 1), :]
                normed[rows, lanes] = (raw * scale).astype(BF16)
        sumsq[b : b + 1, :] += to_lanes(jnp.sum(folded, axis=1, keepdims=True))
    out = more[1][...] if more else None
    for j in range(GROUP):
        cols = pl.ds(pl.multiple_of((at[1] ^ j) * q, LANES), q)
        p = jnp.dot(normed[:, cols], weights[j * q : (j + 1) * q, :], preferred_element_type=F32)
        out = p if out is None else out + p
    acc[...] = out


def part_of(k, rows, blk):
    q = blk.shape[0]
    return jnp.dot(rows[:, k * q : (k + 1) * q], blk[...], preferred_element_type=F32)


def early_kernel(mine, other, a0, b0, out):
    out[...] = part_of(0, mine, a0) + part_of(0, other, b0)


def middle_kernel(mine, total, a1, a2, a3, out):
    acc = total[...]
    for k, blk in enumerate((a1, a2, a3)):
        acc = acc + part_of(k + 1, mine, blk)
    out[...] = acc


def late_kernel(other, total, b1, b2, b3, out_k, out_v):
    head = out_k.shape[1]
    acc = total[...]
    for k, blk in enumerate((b1, b2, b3)):
        acc = acc + part_of(k + 1, other, blk)
    out_k[...] = acc[:, :head].astype(BF16)
    out_v[...] = acc[:, head:].astype(BF16)


def inverse_rms(sqs, full_width):
    sumsq = sqs[0][...]
    for sq in sqs[1:]:
        sumsq = sumsq + sq[...]
    return lax.rsqrt(sumsq / full_width + 1e-05)


def score_kernel(full_width, scale_by, *refs):
    n_off = (len(refs) - 10) // 2
    acc, parts, sqs = refs[0], refs[1 : 1 + n_off], refs[1 + n_off : 2 + 2 * n_off]
    cos, sin, q, room, expo, stats, keys, rows_of = refs[2 + 2 * n_off :]
    tok, head = keys.shape
    window = q.shape[0]
    for j in range(q.shape[1] // head):
        rows_of[j * window : (j + 1) * window, :] = q[:, j * head : (j + 1) * head]
    inv = inverse_rms(sqs, full_width)
    for b in range(tok // LANES):
        rows = pl.ds(b * LANES, LANES)
        k = acc[rows, :head]
        for p in parts:
            k = k + p[rows, :].astype(F32)
        k = k * to_rows(inv[b : b + 1, :], LANES)
        keys[rows, :] = (k * cos[rows, :] + pltpu.roll(k, head // 2, 1) * sin[rows, :]).astype(BF16)
    scores = lax.dot_general(
        keys[...], rows_of[...], (((1,), (1,)), ((), ())), preferred_element_type=F32
    ) * scale_by
    open_to = tok - window
    tail = jnp.where(iota((window, 1), 0) <= room[...], scores[open_to:, :], MASKED)
    body = scores[:open_to, :]
    top = jnp.maximum(
        jnp.max(body, axis=0, keepdims=True), jnp.max(tail, axis=0, keepdims=True)
    )
    body, tail = jnp.exp(body - top), jnp.exp(tail - top)
    expo[:open_to, :] = body
    expo[open_to:, :] = tail
    own = jnp.sum(body, axis=0, keepdims=True) + jnp.sum(tail, axis=0, keepdims=True)
    for d in range(stats.shape[0]):
        stats[d, 0:1, :] = top
        stats[d, 1:2, :] = own


def value_kernel(full_width, *refs):
    n_off = (len(refs) - 3) // 2
    acc, parts, sqs, out = refs[0], refs[1 : 1 + n_off], refs[1 + n_off : 2 + 2 * n_off], refs[-1]
    head = acc.shape[1] // 2
    inv = inverse_rms(sqs, full_width)
    out[...] = jnp.zeros_like(out)
    for b in range(acc.shape[0] // LANES):
        rows = pl.ds(b * LANES, LANES)
        v = acc[rows, head:]
        for p in parts:
            v = v + p[rows, :].astype(F32)
        total = to_lanes(jnp.sum(jnp.abs(v), axis=1, keepdims=True))
        out[b : b + 1, :] = total * (1.0 / head) * inv[b : b + 1, :]


def widen(column, below, above, lane, halfspan):
    pooled = column
    for shift in range(1, REACH + 1):
        right = pltpu.roll(jnp.where(lane < shift, below, column), LANES - shift, 1)
        left = pltpu.roll(jnp.where(lane >= LANES - shift, above, column), shift, 1)
        pooled = jnp.where(
            shift <= halfspan, jnp.maximum(jnp.maximum(pooled, right), left), pooled
        )
    return pooled


def pool_kernel(reach, got, mine, expo, vmag, used, spread):
    tok = expo.shape[0]
    nb = tok // LANES
    row_top = got[0, 0:1, :]
    for d in range(1, got.shape[0]):
        row_top = jnp.maximum(row_top, got[d, 0:1, :])
    row_total = jnp.zeros_like(row_top)
    for d in range(got.shape[0]):
        row_total = row_total + got[d, 1:2, :] * jnp.exp(got[d, 0:1, :] - row_top)
    weight = used[...] * jnp.exp(mine[0, 0:1, :] - row_top) / row_total
    height = vmag.shape[0]
    line = iota((height, LANES), 0)
    lane = iota((height, LANES), 1)
    column = jnp.zeros((height, LANES), F32)
    for b in range(nb):
        mass = jnp.sum(expo[b * LANES : (b + 1) * LANES, :] * weight, axis=1, keepdims=True)
        column = jnp.where(line == b, jnp.broadcast_to(to_lanes(mass), (height, LANES)), column)
    column = column * vmag[...]
    below, above = pltpu.roll(column, height - 1, 0), pltpu.roll(column, 1, 0)
    pooled = widen(column, below, above, lane, reach[...])
    place = line * LANES + lane
    inner = (place >= REACH) & (place < tok - REACH)
    sums = to_lanes(jnp.sum(jnp.where(inner, pooled, 0.0), axis=1, keepdims=True))
    flat = lane[0:1, :]
    last = pltpu.roll(column[nb - 1 : nb, :], 2 * EDGE, 1)
    said = jnp.where(flat < EDGE, column[0:1, :], jnp.where(flat < 2 * EDGE, last, pltpu.roll(sums, 2 * EDGE, 1)))
    spread[...] = jnp.broadcast_to(said, spread.shape)


def rank_kernel(nb, keep, reach, here, said, blocks, share):
    v = said[...]
    n = v.shape[0]
    line, lane = iota(v.shape, 0), iota(v.shape, 1)
    following = pltpu.roll(v, n - 1, 0)
    seam = jnp.where(lane < EDGE, pltpu.roll(v, LANES - EDGE, 1), pltpu.roll(following, EDGE, 1))
    seam = jnp.where(lane < 2 * EDGE, seam, 0.0)
    end = line == n - 1
    apart = LANES // 2
    both = jnp.where(end & (lane >= EDGE), 0.0, seam) + pltpu.roll(
        jnp.where(end & (lane < EDGE), 0.0, seam), apart, 1
    )
    pooled = both
    for shift in range(1, REACH + 1):
        near = jnp.maximum(pltpu.roll(both, shift, 1), pltpu.roll(both, LANES - shift, 1))
        pooled = jnp.where(shift <= reach[...], jnp.maximum(pooled, near), pooled)
    tail = (lane >= EDGE - REACH) & (lane < EDGE)
    lead = (lane >= apart + EDGE) & (lane < apart + EDGE + REACH)
    tail = jnp.sum(jnp.where(tail, pooled, 0.0), axis=1, keepdims=True)
    lead = jnp.sum(jnp.where(lead, pooled, 0.0), axis=1, keepdims=True)
    lead = pltpu.roll(jnp.broadcast_to(lead, v.shape), 1, 0)
    b = pltpu.roll(v, LANES - 2 * EDGE, 1)
    b = b + jnp.where(lane == 0, lead, 0.0) + jnp.where(lane == nb - 1, tail, 0.0)
    b = jnp.where(lane < nb, b, 0.0)
    own = jnp.sum(jnp.where(line == here[...], b, 0.0), axis=0, keepdims=True)
    blocks[...] = own[:, :nb]
    place = line * nb + lane
    rank = jnp.zeros(v.shape, jnp.int32)

    def turned(t, k):
        return jnp.where(lane >= k, pltpu.roll(t, k, 1), pltpu.roll(t, LANES + k - nb, 1)) if k else t

    for k in range(nb):
        bk, pk = turned(b, k), turned(place, k)
        for m in range(n):
            bm, pm = (pltpu.roll(bk, m, 0), pltpu.roll(pk, m, 0)) if m else (bk, pk)
            rank = rank + jnp.where((bm > b) | ((bm == b) & (pm < place)), 1, 0)

    def add(t):
        return jnp.sum(jnp.sum(t, axis=1, keepdims=True), axis=0, keepdims=True)

    kept = jnp.where((lane < nb) & (rank < keep[...]), b, 0.0)
    share[...] = add(kept) / add(b)


def local(
    hidden, gain, key_matrix, value_matrix, queries, window_len, kernel_width, kept_block_count
):
    tok, feats = hidden.shape
    full_width = gain.shape[0]
    head = key_matrix.shape[1]
    n_seq, n_head = lax.axis_size("seq"), lax.axis_size("head")
    n_x = n_head // CORES
    s, h = lax.axis_index("seq"), lax.axis_index("head")
    x, c = h // CORES, h % CORES
    i = s % GROUP
    q = feats // GROUP
    total_tokens = tok * n_seq
    offsets = range(1, n_x)

    def shift_x(offset):
        return [
            (a * CORES + b, (a + offset) % n_x * CORES + b) for a in range(n_x) for b in range(CORES)
        ]

    def flip(bit):
        return [(j, j ^ bit) for j in range(n_seq)]

    def rows_at(start, count):
        return jnp.concatenate(
            [lax.dynamic_slice_in_dim(m, start, count) for m in (key_matrix, value_matrix)], axis=1
        )

    def crossing(block):
        return [
            [
                rows_at(((x - o) % n_x * CORES + (c ^ part)) * feats + block * q, q)
                for part in range(CORES)
            ]
            for o in offsets
        ]

    def cross(rows):
        return [
            [lax.ppermute(rows[o - 1][part], "head", shift_x(-o)) for part in range(CORES)]
            for o in offsets
        ]

    lead = crossing(i)
    lead[0][0], key_matrix, value_matrix = lax.optimization_barrier(
        (lead[0][0], key_matrix, value_matrix)
    )
    firsts = cross([lead[0][:1] + rest[1:] if k == 0 else rest for k, rest in enumerate(crossing(i))])
    seconds = cross(crossing(3 - i))
    own = [rows_at(start * feats, feats) for start in (h, h ^ 1)]
    swapped = lax.ppermute(hidden, "head", [(j, j ^ 1) for j in range(n_head)])
    blocks = [
        [
            [firsts[o - 1][part]]
            + [lax.ppermute(firsts[o - 1][part], "seq", flip(bit)) for bit in (1, 2)]
            + [seconds[o - 1][part]]
            for part in range(CORES)
        ]
        for o in offsets
    ]

    lines = -(-(tok // LANES) // 8) * 8
    gain_lines = gain.reshape(full_width // LANES, LANES)

    def norm(core, rows, own, more):
        return call(
            norm_kernel,
            [sds((tok, feats), BF16), sds((lines, LANES), F32), sds((tok, 2 * head), F32)],
            [SMEM] + [VMEM] * (3 + len(more)),
            flops=1 << 30,
        )(jnp.stack([core * (feats // LANES), i]), rows, gain_lines, own, *more)

    mine, sumsq, acc = norm(h, hidden, own[0], ())

    window = queries.shape[0]
    group_heads = queries.shape[1] // head
    rows = window * group_heads
    row_window = (jnp.arange(rows) % window).astype(jnp.int32)[None, :]
    room = total_tokens - window + row_window - (s * tok + tok - window)
    used = (row_window >= window - window_len[0]).astype(F32)
    reach = jnp.broadcast_to((kernel_width - 1) // 2, (1, LANES))
    keep = jnp.broadcast_to(kept_block_count, (1, LANES))
    here = jnp.broadcast_to(s, (1, LANES)).astype(jnp.int32)
    swapped, room, used, reach = lax.optimization_barrier((swapped, room, used, reach))
    other, sumsq, acc = norm(h ^ 1, swapped, own[1], (sumsq, acc))
    sqs = [sumsq] + [lax.ppermute(sumsq, "head", shift_x(o)) for o in offsets]

    parts_k, parts_v = [], []
    wide, thin = sds((tok, 2 * head), F32), sds((tok, head), BF16)
    for o in offsets:
        half_0, half_1 = blocks[o - 1]
        part = call(early_kernel, wide, [VMEM] * 4, flops=1 << 29)(
            mine, other, half_0[0], half_1[0]
        )
        part = call(middle_kernel, wide, [VMEM] * 5, flops=1 << 29)(mine, part, *half_0[1:])
        part_k, part_v = call(
            late_kernel, [thin, thin], [VMEM] * 5, flops=1 << 29
        )(other, part, *half_1[1:])
        parts_k.append(lax.ppermute(part_k, "head", shift_x(o)))
        parts_v.append(lax.ppermute(part_v, "head", shift_x(o)))

    half = head // 2
    freq = 500000.0 ** (-(jnp.arange(half).astype(F32) * 2.0) / head)
    token = s * tok + jnp.arange(tok)
    angle = token.astype(F32)[:, None] * freq[None, :]
    cos, sin = jnp.cos(angle), jnp.sin(angle)
    cos = jnp.concatenate([cos, cos], axis=1)
    sin = jnp.concatenate([-sin, sin], axis=1)

    expo, stats = call(
        functools.partial(score_kernel, full_width, head ** (-0.5)),
        [sds((tok, rows), F32), sds((n_seq, 2, rows), F32)],
        [VMEM] * (6 + 2 * len(offsets)),
        scratch=[pltpu.VMEM((tok, head), BF16), pltpu.VMEM((rows, head), BF16)],
        flops=1 << 28,
    )(acc, *parts_k, *sqs, cos, sin, queries, room)
    got = lax.all_to_all(stats, "seq", 0, 0, tiled=True)
    nb = tok // BLK
    vmag = call(
        functools.partial(value_kernel, full_width),
        sds((lines, LANES), F32),
        [VMEM] * (2 + 2 * len(offsets)),
        flops=1 << 28,
    )(acc, *parts_v, *sqs)
    spread = call(
        pool_kernel, sds((n_seq, LANES), F32), [VMEM] * 6, flops=1 << 26
    )(reach, got, stats, expo, vmag, used)
    said = lax.all_to_all(spread, "seq", 0, 0, tiled=True)
    local_blocks, fraction = call(
        functools.partial(rank_kernel, nb),
        [sds((1, nb), F32), sds((1, 1), F32)],
        [VMEM] * 4,
        flops=1 << 20,
    )(keep, reach, here, said)
    return (local_blocks, fraction.reshape(1))


def solution(mesh):
    return jax.shard_map(
        local,
        mesh=mesh,
        in_specs=(
            P("seq", "head"),
            P(),
            P(None, "head"),
            P(None, "head"),
            P(None, "head"),
            P("head"),
            P("head"),
            P("head"),
        ),
        out_specs=(P("head", "seq"), P("head")),
        check_vma=False,
    )
```

profile of v0, /device:TPU:0, one launch (start us, length us, event | category | flops | bytes accessed | tf_op | source)
XLA Modules:
  0.0 66.9 jit_solution(5608245181561479523)
XLA Ops:
  1.2 1.0 %constant_dynamic-slice_fusion.10 = (bf16[512,128]{1,0:T(8,128)(2,1)S(1)}, bf16[512,128]{1,0:T(8,128)(2,1)S(1)}) fusion(bf16[8192,128]{1,0:T(8,128)(2,1)} %param.11, s32[]{:T(128)S(6)} %select_n.82, bf16[8192,128]{1,0:T(8,128)(2,1)} %param.10), kind=kLoop, calls=%fused_computation.23 | loop fusion | bytes 524292 | tf_op jit(solution)/shard_map/dynamic_slice | solution.py:273
  2.3 2.7 %collective-permute-start.1 = (bf16[512,256]{1,0:T(8,128)(2,1)S(1)}, bf16[512,256]{1,0:T(8,128)(2,1)S(1)}, u32[]{:S(2)}, u32[]{:S(2)}) collective-permute-start(bf16[512,256]{1,0:T(8,128)(2,1)S(1)} %pad_maximum_fusion.2), channel_id=1, source_target_pairs={{0,2},{1,3},{2,0},{3,1},{4,6},{5,7},{6,4},{7,5},{8,10},{9,11},{10,... | collective-permute-start | bytes 786440 | tf_op jit(solution)/shard_map/ppermute | solution.py:287
  5.0 1.1 %constant_dynamic-slice_fusion = (bf16[512,128]{1,0:T(8,128)(2,1)S(1)}, bf16[512,128]{1,0:T(8,128)(2,1)S(1)}, bf16[512,128]{1,0:T(8,128)(2,1)S(1)}) fusion(bf16[8192,128]{1,0:T(8,128)(2,1)} %param.11, s32[]{:T(128)S(6)} %select_n.87, s32[]{:T(128)S(6)} %select_n.86, s32[]{:T(128)S(6)} %select_n.85), kind=kLoop, calls=%fused_computation.13 | loop fusion | bytes 786444 | tf_op jit(solution)/shard_map/dynamic_slice | solution.py:273
  6.0 1.1 %constant_dynamic-slice_fusion.1 = (bf16[512,128]{1,0:T(8,128)(2,1)S(1)}, bf16[512,128]{1,0:T(8,128)(2,1)S(1)}, bf16[512,128]{1,0:T(8,128)(2,1)S(1)}) fusion(bf16[8192,128]{1,0:T(8,128)(2,1)} %param.10, s32[]{:T(128)S(6)} %select_n.87, s32[]{:T(128)S(6)} %select_n.86, s32[]{:T(128)S(6)} %select_n.85), kind=kLoop, calls=%fused_computation.14 | loop fusion | bytes 786444 | tf_op jit(solution)/shard_map/dynamic_slice | solution.py:273
  8.6 2.0 %collective-permute-start.5 = (bf16[512,256]{1,0:T(8,128)(2,1)}, bf16[512,256]{1,0:T(8,128)(2,1)S(1)}, u32[]{:S(2)}, u32[]{:S(2)}) collective-permute-start(bf16[512,256]{1,0:T(8,128)(2,1)} %pad_maximum_fusion.4), channel_id=1, source_target_pairs={{0,2},{1,3},{2,0},{3,1},{4,6},{5,7},{6,4},{7,5},{8,10},{9,11},{10,... | collective-permute-start | bytes 786440 | tf_op jit(solution)/shard_map/ppermute | solution.py:287
  11.4 1.5 %copy-done.4 = bf16[8192,128]{1,0:T(8,128)(2,1)S(1)} copy-done((bf16[8192,128]{1,0:T(8,128)(2,1)S(1)}, bf16[8192,128]{1,0:T(8,128)(2,1)}, u32[]{:S(2)}) %copy-start.4) | copy-done | bytes 2097176
  13.3 1.6 %collective-permute-start.3 = (bf16[512,256]{1,0:T(8,128)(2,1)S(1)}, bf16[512,256]{1,0:T(8,128)(2,1)S(1)}, u32[]{:S(2)}, u32[]{:S(2)}) collective-permute-start(bf16[512,256]{1,0:T(8,128)(2,1)S(1)} %collective-permute-done.1.a0), channel_id=1, source_target_pairs={{0,4},{4,0},{8,12},{12,8},{16,20},{20,16},{24,28},{28,24},{1,5},{5... | collective-permute-start | bytes 786440 | tf_op jit(solution)/shard_map/ppermute | solution.py:302
  14.9 1.6 %collective-permute-start.4 = (bf16[512,256]{1,0:T(8,128)(2,1)S(1)}, bf16[512,256]{1,0:T(8,128)(2,1)S(1)}, u32[]{:S(2)}, u32[]{:S(2)}) collective-permute-start(bf16[512,256]{1,0:T(8,128)(2,1)S(1)} %collective-permute-done.1.a0), channel_id=1, source_target_pairs={{0,8},{4,12},{8,0},{12,4},{16,24},{20,28},{24,16},{28,20},{1,9},{5... | collective-permute-start | bytes 786440 | tf_op jit(solution)/shard_map/ppermute | solution.py:302
  17.7 2.0 %collective-permute-start.8 = (bf16[512,256]{1,0:T(8,128)(2,1)S(1)}, bf16[512,256]{1,0:T(8,128)(2,1)S(1)}, u32[]{:S(2)}, u32[]{:S(2)}) collective-permute-start(bf16[512,256]{1,0:T(8,128)(2,1)S(1)} %pad_maximum_fusion.5), channel_id=1, source_target_pairs={{0,2},{1,3},{2,0},{3,1},{4,6},{5,7},{6,4},{7,5},{8,10},{9,11},{10,... | collective-permute-start | bytes 786440 | tf_op jit(solution)/shard_map/ppermute | solution.py:287
  19.8 3.6 %collective-permute-done.5.a3 = bf16[512,256]{1,0:T(8,128)(2,1)S(1)} collective-permute-done((bf16[512,256]{1,0:T(8,128)(2,1)}, bf16[512,256]{1,0:T(8,128)(2,1)S(1)}, u32[]{:S(2)}, u32[]{:S(2)}) %collective-permute-start.5) | collective-permute-done | bytes 262176 | tf_op jit(solution)/shard_map/ppermute | solution.py:287
  23.4 2.0 %collective-permute-start.6 = (bf16[512,256]{1,0:T(8,128)(2,1)S(1)}, bf16[512,256]{1,0:T(8,128)(2,1)S(1)}, u32[]{:S(2)}, u32[]{:S(2)}) collective-permute-start(bf16[512,256]{1,0:T(8,128)(2,1)S(1)} %collective-permute-done.2.b0), channel_id=1, source_target_pairs={{0,4},{4,0},{8,12},{12,8},{16,20},{20,16},{24,28},{28,24},{1,5},{5... | collective-permute-start | bytes 786440 | tf_op jit(solution)/shard_map/ppermute | solution.py:302
  25.4 1.6 %collective-permute-start.7 = (bf16[512,256]{1,0:T(8,128)(2,1)S(1)}, bf16[512,256]{1,0:T(8,128)(2,1)S(1)}, u32[]{:S(2)}, u32[]{:S(2)}) collective-permute-start(bf16[512,256]{1,0:T(8,128)(2,1)S(1)} %collective-permute-done.2.b0), channel_id=1, source_target_pairs={{0,8},{4,12},{8,0},{12,4},{16,24},{20,28},{24,16},{28,20},{1,9},{5... | collective-permute-start | bytes 786440 | tf_op jit(solution)/shard_map/ppermute | solution.py:302
  27.0 1.6 %copy-done.1 = bf16[512,2048]{1,0:T(8,128)(2,1)S(1)} copy-done((bf16[512,2048]{1,0:T(8,128)(2,1)S(1)}, bf16[512,2048]{1,0:T(8,128)(2,1)}, u32[]{:S(2)}) %copy-start.1) | copy-done | bytes 2097176
  28.6 2.2 %shard_map.98 = (bf16[512,2048]{1,0:T(8,128)(2,1)S(1)}, f32[8,128]{1,0:T(8,128)S(1)}, f32[512,256]{1,0:T(8,128)S(1)}) custom-call(s32[2]{0:T(128)S(1)} %get-tuple-element.54.at, bf16[512,2048]{1,0:T(8,128)(2,1)S(1)} %copy-done.1, f32[64,128]{1,0:T(8,128)S(1)} %bitcast.14, bf16[2048,256]{1,0:T(8,128)(2,1)S(1)} %pad_maximum_fusion.1.weights), custom_call_target="tpu_custom_call" | custom-call | flops 1073741824 | bytes 1048576 | tf_op jit(solution)/shard_map/pallas_call | solution.py:313
  30.8 3.3 %shard_map.99 = (bf16[512,2048]{1,0:T(8,128)(2,1)S(1)}, f32[8,128]{1,0:T(8,128)S(1)}, f32[512,256]{1,0:T(8,128)S(1)}) custom-call(s32[2]{0:T(128)S(1)} %get-tuple-element.53.at, bf16[512,2048]{1,0:T(8,128)(2,1)} %collective-permute-done.hid, f32[64,128]{1,0:T(8,128)S(1)} %bitcast.15, bf16[2048,256]{1,0:T(8,128)(2,1)S(1)} %pad_maximum_fusion.weights, ...), custom_call_target="tpu_custom_call" | custom-call | flops 1073741824 | bytes 1048576 | tf_op jit(solution)/shard_map/pallas_call | solution.py:313
  35.7 1.6 %collective-permute-start.9 = (bf16[512,128]{1,0:T(8,128)(2,1)S(1)}, bf16[512,128]{1,0:T(8,128)(2,1)S(1)}, u32[]{:S(2)}, u32[]{:S(2)}) collective-permute-start(bf16[512,128]{1,0:T(8,128)(2,1)S(1)} %get-tuple-element.31), channel_id=1, source_target_pairs={{0,2},{1,3},{2,0},{3,1},{4,6},{5,7},{6,4},{7,5},{8,10},{9,11},{10,... | collective-permute-start | bytes 393224 | tf_op jit(solution)/shard_map/ppermute | solution.py:346
  38.9 1.5 %collective-permute-start.11 = (bf16[512,128]{1,0:T(8,128)(2,1)S(1)}, bf16[512,128]{1,0:T(8,128)(2,1)S(1)}, u32[]{:S(2)}, u32[]{:S(2)}) collective-permute-start(bf16[512,128]{1,0:T(8,128)(2,1)S(1)} %get-tuple-element.36), channel_id=1, source_target_pairs={{0,2},{1,3},{2,0},{3,1},{4,6},{5,7},{6,4},{7,5},{8,10},{9,11},{10,... | collective-permute-start | bytes 393224 | tf_op jit(solution)/shard_map/ppermute | solution.py:347
  40.6 1.4 %collective-permute-done.10.refs_3_ = f32[8,128]{1,0:T(8,128)S(1)} collective-permute-done((f32[8,128]{1,0:T(8,128)S(1)}, f32[8,128]{1,0:T(8,128)S(1)}, u32[]{:S(2)}, u32[]{:S(2)}) %collective-permute-start.10) | collective-permute-done | bytes 4128 | tf_op jit(solution)/shard_map/ppermute | solution.py:333
  42.0 1.8 %shard_map.103 = (f32[512,512]{1,0:T(8,128)S(1)}, f32[8,2,512]{2,1,0:T(2,128)}) custom-call(f32[512,256]{1,0:T(8,128)S(1)} %get-tuple-element.27.refs_0_, bf16[512,128]{1,0:T(8,128)(2,1)S(1)} %collective-permute-done.9.refs_1_, f32[8,128]{1,0:T(8,128)S(1)} %get-tuple-element.32.refs_2_, f32[8,128]{1,0:T(8,128)S(1)} %collective-permute-done.10.refs_3_, ...), custom_call_target="tpu_custom_call" | custom-call | flops 268435456 | bytes 1048576 | tf_op jit(solution)/shard_map/pallas_call | solution.py:357
  43.8 3.9 %all-to-all-start = ((f32[8,2,512]{2,1,0:T(2,128)}), f32[8,2,512]{2,1,0:T(2,128)S(1)}, u32[]{:S(2)}, u32[]{:S(2)}) async-start(f32[8,2,512]{2,1,0:T(2,128)} %get-tuple-element.34.mine), calls=%async_computation | async-start | bytes 65536 | tf_op jit(solution)/shard_map/all_to_all | solution.py:364
  47.9 6.5 %all-to-all-done.got = f32[8,2,512]{2,1,0:T(2,128)S(1)} async-done(((f32[8,2,512]{2,1,0:T(2,128)}), f32[8,2,512]{2,1,0:T(2,128)S(1)}, u32[]{:S(2)}, u32[]{:S(2)}) %all-to-all-start) | async-done | bytes 32800 | tf_op jit(solution)/shard_map/all_to_all | solution.py:364
  54.4 1.8 %shard_map.105 = f32[8,128]{1,0:T(8,128)} custom-call(s32[1,128]{1,0:T(1,128)S(1)} %broadcast_in_dim.7.reach, f32[8,2,512]{2,1,0:T(2,128)S(1)} %all-to-all-done.got, f32[8,2,512]{2,1,0:T(2,128)} %get-tuple-element.34.mine, f32[512,512]{1,0:T(8,128)S(1)} %get-tuple-element.35.expo, f32[8,128]{1,0:T(8,128)S(1)} %shard_map.104.vmag, ...), custom_call_target="tpu_custom_call" | custom-call | flops 67108864 | bytes 1048576 | tf_op jit(solution)/shard_map/pallas_call | solution.py:372
  56.2 3.2 %all-to-all-start.1 = ((f32[8,1,128]{2,1,0:T(1,128)}), f32[8,1,128]{2,1,0:T(1,128)S(1)}, u32[]{:S(2)}, u32[]{:S(2)}) async-start(f32[8,1,128]{2,1,0:T(1,128)} %bitcast.8), calls=%async_computation.1 | async-start | bytes 8192 | tf_op jit(solution)/shard_map/all_to_all | solution.py:375
  60.1 5.8 %all-to-all-done.1 = f32[8,1,128]{2,1,0:T(1,128)S(1)} async-done(((f32[8,1,128]{2,1,0:T(1,128)}), f32[8,1,128]{2,1,0:T(1,128)S(1)}, u32[]{:S(2)}, u32[]{:S(2)}) %all-to-all-start.1) | async-done | bytes 4128 | tf_op jit(solution)/shard_map/all_to_all | solution.py:375
  (44 shorter events, 7.8 us)
Async XLA Ops:
  0.6 10.7 %copy-start.3 = (bf16[8192,128]{1,0:T(8,128)(2,1)S(1)}, bf16[8192,128]{1,0:T(8,128)(2,1)}, u32[]{:S(2)}) copy-start(bf16[8192,128]{1,0:T(8,128)(2,1)} %param.11) | copy-start | bytes 6291460
  0.6 24.8 %collective-permute-start = (bf16[512,2048]{1,0:T(8,128)(2,1)}, bf16[512,2048]{1,0:T(8,128)(2,1)}, u32[]{:S(2)}, u32[]{:S(2)}) collective-permute-start(bf16[512,2048]{1,0:T(8,128)(2,1)} %hid.1), channel_id=1, source_target_pairs={{0,1},{1,0},{2,3},{3,2},{4,5},{5,4},{6,7},{7,6},{8,9},{9,8},{10,11... | collective-permute-start | bytes 6291464 | tf_op jit(solution)/shard_map/ppermute | solution.py:298
  2.3 11.0 %collective-permute-start.1 = (bf16[512,256]{1,0:T(8,128)(2,1)S(1)}, bf16[512,256]{1,0:T(8,128)(2,1)S(1)}, u32[]{:S(2)}, u32[]{:S(2)}) collective-permute-start(bf16[512,256]{1,0:T(8,128)(2,1)S(1)} %pad_maximum_fusion.2), channel_id=1, source_target_pairs={{0,2},{1,3},{2,0},{3,1},{4,6},{5,7},{6,4},{7,5},{8,10},{9,11},{10,... | collective-permute-start | bytes 786440 | tf_op jit(solution)/shard_map/ppermute | solution.py:287
  7.8 9.9 %collective-permute-start.2 = (bf16[512,256]{1,0:T(8,128)(2,1)}, bf16[512,256]{1,0:T(8,128)(2,1)S(1)}, u32[]{:S(2)}, u32[]{:S(2)}) collective-permute-start(bf16[512,256]{1,0:T(8,128)(2,1)} %pad_maximum_fusion.3), channel_id=1, source_target_pairs={{0,2},{1,3},{2,0},{3,1},{4,6},{5,7},{6,4},{7,5},{8,10},{9,11},{10,... | collective-permute-start | bytes 786440 | tf_op jit(solution)/shard_map/ppermute | solution.py:287
  8.6 14.7 %collective-permute-start.5 = (bf16[512,256]{1,0:T(8,128)(2,1)}, bf16[512,256]{1,0:T(8,128)(2,1)S(1)}, u32[]{:S(2)}, u32[]{:S(2)}) collective-permute-start(bf16[512,256]{1,0:T(8,128)(2,1)} %pad_maximum_fusion.4), channel_id=1, source_target_pairs={{0,2},{1,3},{2,0},{3,1},{4,6},{5,7},{6,4},{7,5},{8,10},{9,11},{10,... | collective-permute-start | bytes 786440 | tf_op jit(solution)/shard_map/ppermute | solution.py:287
  11.3 1.6 %copy-start.4 = (bf16[8192,128]{1,0:T(8,128)(2,1)S(1)}, bf16[8192,128]{1,0:T(8,128)(2,1)}, u32[]{:S(2)}) copy-start(bf16[8192,128]{1,0:T(8,128)(2,1)} %param.10) | copy-start | bytes 6291460
  12.9 14.1 %copy-start.2 = (f32[8192]{0:T(1024)S(1)}, f32[8192]{0:T(1024)}, u32[]{:S(2)}) copy-start(f32[8192]{0:T(1024)} %param.9) | copy-start | bytes 98308
  13.3 21.2 %collective-permute-start.3 = (bf16[512,256]{1,0:T(8,128)(2,1)S(1)}, bf16[512,256]{1,0:T(8,128)(2,1)S(1)}, u32[]{:S(2)}, u32[]{:S(2)}) collective-permute-start(bf16[512,256]{1,0:T(8,128)(2,1)S(1)} %collective-permute-done.1.a0), channel_id=1, source_target_pairs={{0,4},{4,0},{8,12},{12,8},{16,20},{20,16},{24,28},{28,24},{1,5},{5... | collective-permute-start | bytes 786440 | tf_op jit(solution)/shard_map/ppermute | solution.py:302
  14.9 19.6 %collective-permute-start.4 = (bf16[512,256]{1,0:T(8,128)(2,1)S(1)}, bf16[512,256]{1,0:T(8,128)(2,1)S(1)}, u32[]{:S(2)}, u32[]{:S(2)}) collective-permute-start(bf16[512,256]{1,0:T(8,128)(2,1)S(1)} %collective-permute-done.1.a0), channel_id=1, source_target_pairs={{0,8},{4,12},{8,0},{12,4},{16,24},{20,28},{24,16},{28,20},{1,9},{5... | collective-permute-start | bytes 786440 | tf_op jit(solution)/shard_map/ppermute | solution.py:302
  17.7 17.4 %collective-permute-start.8 = (bf16[512,256]{1,0:T(8,128)(2,1)S(1)}, bf16[512,256]{1,0:T(8,128)(2,1)S(1)}, u32[]{:S(2)}, u32[]{:S(2)}) collective-permute-start(bf16[512,256]{1,0:T(8,128)(2,1)S(1)} %pad_maximum_fusion.5), channel_id=1, source_target_pairs={{0,2},{1,3},{2,0},{3,1},{4,6},{5,7},{6,4},{7,5},{8,10},{9,11},{10,... | collective-permute-start | bytes 786440 | tf_op jit(solution)/shard_map/ppermute | solution.py:287
  23.4 11.8 %collective-permute-start.6 = (bf16[512,256]{1,0:T(8,128)(2,1)S(1)}, bf16[512,256]{1,0:T(8,128)(2,1)S(1)}, u32[]{:S(2)}, u32[]{:S(2)}) collective-permute-start(bf16[512,256]{1,0:T(8,128)(2,1)S(1)} %collective-permute-done.2.b0), channel_id=1, source_target_pairs={{0,4},{4,0},{8,12},{12,8},{16,20},{20,16},{24,28},{28,24},{1,5},{5... | collective-permute-start | bytes 786440 | tf_op jit(solution)/shard_map/ppermute | solution.py:302
  25.4 9.7 %collective-permute-start.7 = (bf16[512,256]{1,0:T(8,128)(2,1)S(1)}, bf16[512,256]{1,0:T(8,128)(2,1)S(1)}, u32[]{:S(2)}, u32[]{:S(2)}) collective-permute-start(bf16[512,256]{1,0:T(8,128)(2,1)S(1)} %collective-permute-done.2.b0), channel_id=1, source_target_pairs={{0,8},{4,12},{8,0},{12,4},{16,24},{20,28},{24,16},{28,20},{1,9},{5... | collective-permute-start | bytes 786440 | tf_op jit(solution)/shard_map/ppermute | solution.py:302
  27.0 1.6 %copy-start.1 = (bf16[512,2048]{1,0:T(8,128)(2,1)S(1)}, bf16[512,2048]{1,0:T(8,128)(2,1)}, u32[]{:S(2)}) copy-start(bf16[512,2048]{1,0:T(8,128)(2,1)} %hid.1) | copy-start | bytes 6291460
  35.1 6.9 %copy-start = (bf16[64,1024]{1,0:T(8,128)(2,1)S(1)}, bf16[64,1024]{1,0:T(8,128)(2,1)}, u32[]{:S(2)}) copy-start(bf16[64,1024]{1,0:T(8,128)(2,1)} %refs_6_.1) | copy-start | bytes 393220
  35.7 6.3 %collective-permute-start.9 = (bf16[512,128]{1,0:T(8,128)(2,1)S(1)}, bf16[512,128]{1,0:T(8,128)(2,1)S(1)}, u32[]{:S(2)}, u32[]{:S(2)}) collective-permute-start(bf16[512,128]{1,0:T(8,128)(2,1)S(1)} %get-tuple-element.31), channel_id=1, source_target_pairs={{0,2},{1,3},{2,0},{3,1},{4,6},{5,7},{6,4},{7,5},{8,10},{9,11},{10,... | collective-permute-start | bytes 393224 | tf_op jit(solution)/shard_map/ppermute | solution.py:346
  38.3 3.7 %collective-permute-start.10 = (f32[8,128]{1,0:T(8,128)S(1)}, f32[8,128]{1,0:T(8,128)S(1)}, u32[]{:S(2)}, u32[]{:S(2)}) collective-permute-start(f32[8,128]{1,0:T(8,128)S(1)} %get-tuple-element.32.refs_2_), channel_id=1, source_target_pairs={{0,2},{1,3},{2,0},{3,1},{4,6},{5,7},{6,4},{7,5},{8,10},{9,11},{10,... | collective-permute-start | bytes 12296 | tf_op jit(solution)/shard_map/ppermute | solution.py:333
  38.9 8.8 %collective-permute-start.11 = (bf16[512,128]{1,0:T(8,128)(2,1)S(1)}, bf16[512,128]{1,0:T(8,128)(2,1)S(1)}, u32[]{:S(2)}, u32[]{:S(2)}) collective-permute-start(bf16[512,128]{1,0:T(8,128)(2,1)S(1)} %get-tuple-element.36), channel_id=1, source_target_pairs={{0,2},{1,3},{2,0},{3,1},{4,6},{5,7},{6,4},{7,5},{8,10},{9,11},{10,... | collective-permute-start | bytes 393224 | tf_op jit(solution)/shard_map/ppermute | solution.py:347
  43.8 10.6 %all-to-all-start = ((f32[8,2,512]{2,1,0:T(2,128)}), f32[8,2,512]{2,1,0:T(2,128)S(1)}, u32[]{:S(2)}, u32[]{:S(2)}) async-start(f32[8,2,512]{2,1,0:T(2,128)} %get-tuple-element.34.mine), calls=%async_computation | async-start | bytes 65536 | tf_op jit(solution)/shard_map/all_to_all | solution.py:364
  56.2 9.7 %all-to-all-start.1 = ((f32[8,1,128]{2,1,0:T(1,128)}), f32[8,1,128]{2,1,0:T(1,128)S(1)}, u32[]{:S(2)}, u32[]{:S(2)}) async-start(f32[8,1,128]{2,1,0:T(1,128)} %bitcast.8), calls=%async_computation.1 | async-start | bytes 8192 | tf_op jit(solution)/shard_map/all_to_all | solution.py:375
where the time goes:
time: 67.3 us; the launch traced here: 66.9 us
  starting transfers between devices  24.8 us (37%)
  waiting for transfers between devices  17.9 us (27%)
  Pallas kernels  11.8 us (18%)
  local copies, waits for them, and re-layouts  6.4 us (10%)
  other arithmetic  3.09 us (5%)
  between operations  2.86 us (4%)
    ppermute x4, starting transfers between devices, local(): lax.ppermute(firsts[o - 1][part], 'seq', flip(bit))  6.79 us
    ppermute x4, starting transfers between devices, cross(): lax.ppermute(rows[o - 1][part], 'head', shift_x(-o))  6.72 us
    all_to_all x1, waiting for transfers between devices, local(): got = lax.all_to_all(stats, 'seq', 0, 0, tiled=True)  6.51 us
    all_to_all x1, waiting for transfers between devices, local(): said = lax.all_to_all(spread, 'seq', 0, 0, tiled=True)  5.78 us
    pallas_call x2, Pallas kernels, norm(): call(norm_kernel, [sds((tok, feats), BF16), sds((lines, LANES), F32), sds...  5.44 us
    ppermute x4, waiting for transfers between devices, cross(): lax.ppermute(rows[o - 1][part], 'head', shift_x(-o))  4.15 us
    all_to_all x1, starting transfers between devices, local(): got = lax.all_to_all(stats, 'seq', 0, 0, tiled=True)  3.87 us
    dynamic_slice x5, local copies, waits for them, and re-layouts, rows_at(): lax.dynamic_slice_in_dim(m, start, count)  3.32 us
  transfers between devices with their start and end apart: 14, of which 5 were waited for; matrix products, arithmetic and copies ran while one was open for 10% of the time, Pallas kernels for 13%

commit v1 on v0

--- a/solution.py
+++ b/solution.py
@@ -260,10 +260,8 @@
     total_tokens = tok * n_seq
     offsets = range(1, n_x)
 
-    def shift_x(offset):
-        return [
-            (a * CORES + b, (a + offset) % n_x * CORES + b) for a in range(n_x) for b in range(CORES)
-        ]
+    def shift_x(offset, cores=range(CORES)):
+        return [(a * CORES + b, (a + offset) % n_x * CORES + b) for a in range(n_x) for b in cores]
 
     def flip(bit):
         return [(j, j ^ bit) for j in range(n_seq)]
@@ -282,9 +280,17 @@
             for o in offsets
         ]
 
-    def cross(rows):
+    def piece(name, part, o, rows, following):
+        if name != "first" or part:
+            return lax.ppermute(rows, "head", shift_x(-o))
+        later, following[1] = lax.optimization_barrier((rows, following[1]))
+        ahead = lax.ppermute(rows, "head", shift_x(-o, (0,)))
+        behind = lax.ppermute(later, "head", shift_x(-o, (1,)))
+        return jnp.where(c == 0, ahead, behind)
+
+    def cross(name, rows):
         return [
-            [lax.ppermute(rows[o - 1][part], "head", shift_x(-o)) for part in range(CORES)]
+            [piece(name, part, o, rows[o - 1][part], rows[o - 1]) for part in range(CORES)]
             for o in offsets
         ]
 
@@ -292,8 +298,8 @@
     lead[0][0], key_matrix, value_matrix = lax.optimization_barrier(
         (lead[0][0], key_matrix, value_matrix)
     )
-    firsts = cross([lead[0][:1] + rest[1:] if k == 0 else rest for k, rest in enumerate(crossing(i))])
-    seconds = cross(crossing(3 - i))
+    firsts = cross("first", [lead[0][:1] + rest[1:] if k == 0 else rest for k, rest in enumerate(crossing(i))])
+    seconds = cross("second", crossing(3 - i))
     own = [rows_at(start * feats, feats) for start in (h, h ^ 1)]
     swapped = lax.ppermute(hidden, "head", [(j, j ^ 1) for j in range(n_head)])
     blocks = [
@@ -328,7 +334,9 @@
     reach = jnp.broadcast_to((kernel_width - 1) // 2, (1, LANES))
     keep = jnp.broadcast_to(kept_block_count, (1, LANES))
     here = jnp.broadcast_to(s, (1, LANES)).astype(jnp.int32)
-    swapped, room, used, reach = lax.optimization_barrier((swapped, room, used, reach))
+    swapped, room, used, reach, keep, here = lax.optimization_barrier(
+        (swapped, room, used, reach, keep, here)
+    )
     other, sumsq, acc = norm(h ^ 1, swapped, own[1], (sumsq, acc))
     sqs = [sumsq] + [lax.ppermute(sumsq, "head", shift_x(o)) for o in offsets]
 

time: 67.3 us -> 67 us (level)
  blocking collectives: 0 us -> 8.86 us
  waiting for transfers between devices: 17.9 us -> 12.5 us
  starting transfers between devices: 24.8 us -> 22 us
  Pallas kernels: 11.8 us -> 11.1 us
  local copies, waits for them, and re-layouts: 6.4 us -> 5.7 us
    all_to_all x0 -> x1, blocking collectives: none -> 8.86 us  [local(): said = lax.all_to_all(spread, 'seq', 0, 0, tiled=True)]
    all_to_all x1 -> x0, waiting for transfers between devices: 5.78 us -> none  [local(): said = lax.all_to_all(spread, 'seq', 0, 0, tiled=True)]
    all_to_all x1 -> x0, starting transfers between devices: 3.25 us -> none  [local(): said = lax.all_to_all(spread, 'seq', 0, 0, tiled=True)]
    unnamed x10 -> x6, local copies, waits for them, and re-layouts: 3.07 us -> 0.02 us
    dynamic_slice x5, local copies, waits for them, and re-layouts: 3.32 us -> 5.67 us  [rows_at(): lax.dynamic_slice_in_dim(m, start, count)]
    ppermute x4 -> x5, waiting for transfers between devices: 4.15 us -> 2.16 us  [the longest x3 2.15 us: piece(): return lax.ppermute(rows, 'head', shift_x(-o))]
    ppermute x4 -> x5, starting transfers between devices: 6.72 us -> 8.46 us  [the longest x1 4.46 us: piece(): ahead = lax.ppermute(rows, 'head', shift_x(-o, (0,)))]
    ppermute x1, waiting for transfers between devices: 1.43 us -> 3.05 us  [local(): sqs = [sumsq] + [lax.ppermute(sumsq, 'head', shift_x(o)) for o in offsets]]
  transfers between devices with their start and end apart: 14 -> 14, of which waited for: 5 -> 4; matrix products, arithmetic and copies ran while one was open for 10% -> 14% of each run, Pallas kernels for 13% -> 13%
where the time goes in v1:
time: 67 us; the launch traced here: 66.5 us
  starting transfers between devices  22 us (33%)
  waiting for transfers between devices  12.5 us (19%)
  Pallas kernels  11.1 us (17%)
  blocking collectives  8.86 us (13%)
  local copies, waits for them, and re-layouts  5.7 us (9%)
  other arithmetic  3.49 us (5%)
  between operations  2.9 us (4%)
    all_to_all x1, blocking collectives, local(): said = lax.all_to_all(spread, 'seq', 0, 0, tiled=True)  8.86 us
    all_to_all x1, waiting for transfers between devices, local(): got = lax.all_to_all(stats, 'seq', 0, 0, tiled=True)  6.51 us
    ppermute x4, starting transfers between devices, local(): lax.ppermute(firsts[o - 1][part], 'seq', flip(bit))  6.26 us
    dynamic_slice x5, local copies, waits for them, and re-layouts, rows_at(): lax.dynamic_slice_in_dim(m, start, count)  5.67 us
    pallas_call x2, Pallas kernels, norm(): call(norm_kernel, [sds((tok, feats), BF16), sds((lines, LANES), F32), sds...  5.36 us
    all_to_all x1, starting transfers between devices, local(): got = lax.all_to_all(stats, 'seq', 0, 0, tiled=True)  4.5 us
    ppermute x1, starting transfers between devices, piece(): ahead = lax.ppermute(rows, 'head', shift_x(-o, (0,)))  4.46 us
    ppermute x1, waiting for transfers between devices, local(): sqs = [sumsq] + [lax.ppermute(sumsq, 'head', shift_x(o)) for o in offsets]  3.05 us
  transfers between devices with their start and end apart: 14, of which 4 were waited for; matrix products, arithmetic and copies ran while one was open for 14% of the time, Pallas kernels for 13%

profile of v1, /device:TPU:0, one launch (start us, length us, event | category | flops | bytes accessed | tf_op | source)
XLA Modules:
  0.0 66.5 jit_solution(14386191466140721270)
XLA Ops:
  2.2 4.5 %collective-permute-start.1 = (bf16[512,256]{1,0:T(8,128)(2,1)S(1)}, bf16[512,256]{1,0:T(8,128)(2,1)}, u32[]{:S(2)}, u32[]{:S(2)}) collective-permute-start(bf16[512,256]{1,0:T(8,128)(2,1)S(1)} %pad_maximum_fusion.2), channel_id=1, source_target_pairs={{0,2},{2,0},{4,6},{6,4},{8,10},{10,8},{12,14},{14,12},{16,18},{18,... | collective-permute-start | bytes 786440 | tf_op jit(solution)/shard_map/ppermute | solution.py:287
  6.7 1.1 %constant_dynamic-slice_fusion = (bf16[512,128]{1,0:T(8,128)(2,1)S(1)}, bf16[512,128]{1,0:T(8,128)(2,1)S(1)}, bf16[512,128]{1,0:T(8,128)(2,1)S(1)}) fusion(bf16[8192,128]{1,0:T(8,128)(2,1)} %param.11, s32[]{:T(128)S(6)} %select_n.97, s32[]{:T(128)S(6)} %select_n.96, s32[]{:T(128)S(6)} %select_n.94), kind=kLoop, calls=%fused_computation.14 | loop fusion | bytes 786444 | tf_op jit(solution)/shard_map/dynamic_slice | solution.py:271
  7.8 1.1 %constant_dynamic-slice_fusion.1 = (bf16[512,128]{1,0:T(8,128)(2,1)S(1)}, bf16[512,128]{1,0:T(8,128)(2,1)S(1)}, bf16[512,128]{1,0:T(8,128)(2,1)S(1)}) fusion(bf16[8192,128]{1,0:T(8,128)(2,1)} %param.10, s32[]{:T(128)S(6)} %select_n.97, s32[]{:T(128)S(6)} %select_n.96, s32[]{:T(128)S(6)} %select_n.94), kind=kLoop, calls=%fused_computation.15 | loop fusion | bytes 786444 | tf_op jit(solution)/shard_map/dynamic_slice | solution.py:271
  8.9 1.4 %collective-permute-start.2 = (bf16[512,256]{1,0:T(8,128)(2,1)S(1)}, bf16[512,256]{1,0:T(8,128)(2,1)}, u32[]{:S(2)}, u32[]{:S(2)}) collective-permute-start(bf16[512,256]{1,0:T(8,128)(2,1)S(1)} %pad_maximum_fusion.2), channel_id=1, source_target_pairs={{1,3},{3,1},{5,7},{7,5},{9,11},{11,9},{13,15},{15,13},{17,19},{19,... | collective-permute-start | bytes 786440 | tf_op jit(solution)/shard_map/ppermute | solution.py:288
  11.0 2.0 %collective-permute-start.6 = (bf16[512,256]{1,0:T(8,128)(2,1)}, bf16[512,256]{1,0:T(8,128)(2,1)S(1)}, u32[]{:S(2)}, u32[]{:S(2)}) collective-permute-start(bf16[512,256]{1,0:T(8,128)(2,1)} %pad_maximum_fusion.4), channel_id=1, source_target_pairs={{0,2},{1,3},{2,0},{3,1},{4,6},{5,7},{6,4},{7,5},{8,10},{9,11},{10,... | collective-permute-start | bytes 786440 | tf_op jit(solution)/shard_map/ppermute | solution.py:285
  13.8 1.3 %constant_dynamic-slice_fusion.6 = (bf16[2048,128]{1,0:T(8,128)(2,1)S(1)}, bf16[2048,128]{1,0:T(8,128)(2,1)S(1)}) fusion(bf16[8192,128]{1,0:T(8,128)(2,1)} %param.11, s32[]{:T(128)S(6)} %select_n.92, s32[]{:T(128)S(6)} %select_n.91), kind=kLoop, calls=%fused_computation.20 | loop fusion | bytes 2097160 | tf_op jit(solution)/shard_map/dynamic_slice | solution.py:271
  15.1 1.3 %constant_dynamic-slice_fusion.7 = (bf16[2048,128]{1,0:T(8,128)(2,1)S(1)}, bf16[2048,128]{1,0:T(8,128)(2,1)S(1)}) fusion(bf16[8192,128]{1,0:T(8,128)(2,1)} %param.10, s32[]{:T(128)S(6)} %select_n.92, s32[]{:T(128)S(6)} %select_n.91), kind=kLoop, calls=%fused_computation.21 | loop fusion | bytes 2097160 | tf_op jit(solution)/shard_map/dynamic_slice | solution.py:271
  16.7 1.1 %broadcast_select_fusion.a0 = bf16[512,256]{1,0:T(8,128)(2,1)S(1)} fusion(bf16[512,256]{1,0:T(8,128)(2,1)} %collective-permute-done.1, bf16[512,256]{1,0:T(8,128)(2,1)} %collective-permute-done.2, pred[]{:T(512)S(6)} %eq.12), kind=kLoop, calls=%fused_computation.10 | loop fusion | flops 131072 | bytes 786433 | tf_op jit(solution)/shard_map/jit(_where)/select_n | solution.py:289
  17.8 1.6 %collective-permute-start.4 = (bf16[512,256]{1,0:T(8,128)(2,1)S(1)}, bf16[512,256]{1,0:T(8,128)(2,1)S(1)}, u32[]{:S(2)}, u32[]{:S(2)}) collective-permute-start(bf16[512,256]{1,0:T(8,128)(2,1)S(1)} %broadcast_select_fusion.a0), channel_id=1, source_target_pairs={{0,4},{4,0},{8,12},{12,8},{16,20},{20,16},{24,28},{28,24},{1,5},{5... | collective-permute-start | bytes 786440 | tf_op jit(solution)/shard_map/ppermute | solution.py:308
  19.4 1.6 %collective-permute-start.5 = (bf16[512,256]{1,0:T(8,128)(2,1)S(1)}, bf16[512,256]{1,0:T(8,128)(2,1)S(1)}, u32[]{:S(2)}, u32[]{:S(2)}) collective-permute-start(bf16[512,256]{1,0:T(8,128)(2,1)S(1)} %broadcast_select_fusion.a0), channel_id=1, source_target_pairs={{0,8},{4,12},{8,0},{12,4},{16,24},{20,28},{24,16},{28,20},{1,9},{5... | collective-permute-start | bytes 786440 | tf_op jit(solution)/shard_map/ppermute | solution.py:308
  22.9 2.1 %collective-permute-done.6.a3 = bf16[512,256]{1,0:T(8,128)(2,1)S(1)} collective-permute-done((bf16[512,256]{1,0:T(8,128)(2,1)}, bf16[512,256]{1,0:T(8,128)(2,1)S(1)}, u32[]{:S(2)}, u32[]{:S(2)}) %collective-permute-start.6) | collective-permute-done | bytes 262176 | tf_op jit(solution)/shard_map/ppermute | solution.py:285
  25.1 1.5 %collective-permute-start.7 = (bf16[512,256]{1,0:T(8,128)(2,1)S(1)}, bf16[512,256]{1,0:T(8,128)(2,1)S(1)}, u32[]{:S(2)}, u32[]{:S(2)}) collective-permute-start(bf16[512,256]{1,0:T(8,128)(2,1)S(1)} %collective-permute-done.3.b0), channel_id=1, source_target_pairs={{0,4},{4,0},{8,12},{12,8},{16,20},{20,16},{24,28},{28,24},{1,5},{5... | collective-permute-start | bytes 786440 | tf_op jit(solution)/shard_map/ppermute | solution.py:308
  26.6 1.6 %collective-permute-start.8 = (bf16[512,256]{1,0:T(8,128)(2,1)S(1)}, bf16[512,256]{1,0:T(8,128)(2,1)S(1)}, u32[]{:S(2)}, u32[]{:S(2)}) collective-permute-start(bf16[512,256]{1,0:T(8,128)(2,1)S(1)} %collective-permute-done.3.b0), channel_id=1, source_target_pairs={{0,8},{4,12},{8,0},{12,4},{16,24},{20,28},{24,16},{28,20},{1,9},{5... | collective-permute-start | bytes 786440 | tf_op jit(solution)/shard_map/ppermute | solution.py:308
  28.2 2.1 %shard_map.98 = (bf16[512,2048]{1,0:T(8,128)(2,1)S(1)}, f32[8,128]{1,0:T(8,128)S(1)}, f32[512,256]{1,0:T(8,128)S(1)}) custom-call(s32[2]{0:T(128)S(1)} %get-tuple-element.62.at, bf16[512,2048]{1,0:T(8,128)(2,1)S(1)} %copy-done.1, f32[64,128]{1,0:T(8,128)S(1)} %bitcast.15, bf16[2048,256]{1,0:T(8,128)(2,1)S(1)} %pad_maximum_fusion.1.weights), custom_call_target="tpu_custom_call" | custom-call | flops 1073741824 | bytes 1048576 | tf_op jit(solution)/shard_map/pallas_call | solution.py:319
  30.4 3.2 %shard_map.99 = (bf16[512,2048]{1,0:T(8,128)(2,1)S(1)}, f32[8,128]{1,0:T(8,128)S(1)}, f32[512,256]{1,0:T(8,128)S(1)}) custom-call(s32[2]{0:T(128)S(1)} %get-tuple-element.61.at, bf16[512,2048]{1,0:T(8,128)(2,1)} %collective-permute-done.hid, f32[64,128]{1,0:T(8,128)S(1)} %bitcast.16, bf16[2048,256]{1,0:T(8,128)(2,1)S(1)} %pad_maximum_fusion.weights, ...), custom_call_target="tpu_custom_call" | custom-call | flops 1073741824 | bytes 1048576 | tf_op jit(solution)/shard_map/pallas_call | solution.py:319
  36.1 1.0 %fusion = (f32[512,64]{1,0:T(8,128)S(1)}, f32[512,64]{1,0:T(8,128)S(1)}, f32[512,64]{1,0:T(8,128)S(1)}) fusion(f32[64]{0:T(128)S(1)} %multiply_power_fusion, f32[512]{0:T(512)S(1)} %add_convert_fusion), kind=kLoop, calls=%fused_computation.11 | loop fusion | flops 65536 | bytes 395520 | tf_op jit(solution)/shard_map/neg | solution.py:363
  37.0 2.1 %collective-permute-start.11 = (f32[8,128]{1,0:T(8,128)S(1)}, f32[8,128]{1,0:T(8,128)S(1)}, u32[]{:S(2)}, u32[]{:S(2)}) collective-permute-start(f32[8,128]{1,0:T(8,128)S(1)} %get-tuple-element.40.refs_2_), channel_id=1, source_target_pairs={{0,2},{1,3},{2,0},{3,1},{4,6},{5,7},{6,4},{7,5},{8,10},{9,11},{10,... | collective-permute-start | bytes 12296 | tf_op jit(solution)/shard_map/ppermute | solution.py:341
  39.4 3.1 %collective-permute-done.11.refs_3_ = f32[8,128]{1,0:T(8,128)S(1)} collective-permute-done((f32[8,128]{1,0:T(8,128)S(1)}, f32[8,128]{1,0:T(8,128)S(1)}, u32[]{:S(2)}, u32[]{:S(2)}) %collective-permute-start.11) | collective-permute-done | bytes 4128 | tf_op jit(solution)/shard_map/ppermute | solution.py:341
  42.5 1.8 %shard_map.103 = (f32[512,512]{1,0:T(8,128)S(1)}, f32[8,2,512]{2,1,0:T(2,128)}) custom-call(f32[512,256]{1,0:T(8,128)S(1)} %get-tuple-element.33.refs_0_, bf16[512,128]{1,0:T(8,128)(2,1)S(1)} %collective-permute-done.10.refs_1_, f32[8,128]{1,0:T(8,128)S(1)} %get-tuple-element.40.refs_2_, f32[8,128]{1,0:T(8,128)S(1)} %collective-permute-done.11.refs_3_, ...), custom_call_target="tpu_custom_call" | custom-call | flops 268435456 | bytes 1048576 | tf_op jit(solution)/shard_map/pallas_call | solution.py:365
  44.3 4.5 %all-to-all-start = ((f32[8,2,512]{2,1,0:T(2,128)}), f32[8,2,512]{2,1,0:T(2,128)S(1)}, u32[]{:S(2)}, u32[]{:S(2)}) async-start(f32[8,2,512]{2,1,0:T(2,128)} %get-tuple-element.42.mine), calls=%async_computation | async-start | bytes 65536 | tf_op jit(solution)/shard_map/all_to_all | solution.py:372
  49.0 6.5 %all-to-all-done.got = f32[8,2,512]{2,1,0:T(2,128)S(1)} async-done(((f32[8,2,512]{2,1,0:T(2,128)}), f32[8,2,512]{2,1,0:T(2,128)S(1)}, u32[]{:S(2)}, u32[]{:S(2)}) %all-to-all-start) | async-done | bytes 32800 | tf_op jit(solution)/shard_map/all_to_all | solution.py:372
  55.5 1.2 %shard_map.105 = f32[8,128]{1,0:T(8,128)S(1)} custom-call(s32[1,128]{1,0:T(1,128)S(1)} %broadcast_in_dim.6.reach, f32[8,2,512]{2,1,0:T(2,128)S(1)} %all-to-all-done.got, f32[8,2,512]{2,1,0:T(2,128)} %get-tuple-element.42.mine, f32[512,512]{1,0:T(8,128)S(1)} %get-tuple-element.43.expo, f32[8,128]{1,0:T(8,128)S(1)} %shard_map.104.vmag, ...), custom_call_target="tpu_custom_call" | custom-call | flops 67108864 | bytes 1048576 | tf_op jit(solution)/shard_map/pallas_call | solution.py:380
  56.6 8.9 %all_to_all.16 = f32[8,1,128]{2,1,0:T(1,128)S(1)} all-to-all(f32[8,1,128]{2,1,0:T(1,128)S(1)} %bitcast.13), channel_id=1, replica_groups=mesh['seq'=8,'head'=4] {'seq'}, dimensions={0} | all-to-all | bytes 8192 | tf_op jit(solution)/shard_map/all_to_all | solution.py:383
  65.5 1.0 %shard_map.106 = (f32[1,4]{1,0:T(1,128)}, f32[1,1]{1,0:T(1,128)}) custom-call(s32[1,128]{1,0:T(1,128)S(1)} %broadcast_in_dim.7.keep, s32[1,128]{1,0:T(1,128)S(1)} %broadcast_in_dim.6.reach, s32[1,128]{1,0:T(1,128)S(1)} %broadcast_in_dim.8.here, f32[8,128]{1,0:T(8,128)S(1)} %bitcast.14), custom_call_target="tpu_custom_call" | custom-call | flops 1048576 | bytes 1048576 | tf_op jit(solution)/shard_map/pallas_call | solution.py:384
  (42 shorter events, 6.2 us)
Async XLA Ops:
  0.6 26.0 %collective-permute-start = (bf16[512,2048]{1,0:T(8,128)(2,1)}, bf16[512,2048]{1,0:T(8,128)(2,1)}, u32[]{:S(2)}, u32[]{:S(2)}) collective-permute-start(bf16[512,2048]{1,0:T(8,128)(2,1)} %hid.1), channel_id=1, source_target_pairs={{0,1},{1,0},{2,3},{3,2},{4,5},{5,4},{6,7},{7,6},{8,9},{9,8},{10,11... | collective-permute-start | bytes 6291464 | tf_op jit(solution)/shard_map/ppermute | solution.py:304
  2.2 14.5 %collective-permute-start.1 = (bf16[512,256]{1,0:T(8,128)(2,1)S(1)}, bf16[512,256]{1,0:T(8,128)(2,1)}, u32[]{:S(2)}, u32[]{:S(2)}) collective-permute-start(bf16[512,256]{1,0:T(8,128)(2,1)S(1)} %pad_maximum_fusion.2), channel_id=1, source_target_pairs={{0,2},{2,0},{4,6},{6,4},{8,10},{10,8},{12,14},{14,12},{16,18},{18,... | collective-permute-start | bytes 786440 | tf_op jit(solution)/shard_map/ppermute | solution.py:287
  8.9 7.8 %collective-permute-start.2 = (bf16[512,256]{1,0:T(8,128)(2,1)S(1)}, bf16[512,256]{1,0:T(8,128)(2,1)}, u32[]{:S(2)}, u32[]{:S(2)}) collective-permute-start(bf16[512,256]{1,0:T(8,128)(2,1)S(1)} %pad_maximum_fusion.2), channel_id=1, source_target_pairs={{1,3},{3,1},{5,7},{7,5},{9,11},{11,9},{13,15},{15,13},{17,19},{19,... | collective-permute-start | bytes 786440 | tf_op jit(solution)/shard_map/ppermute | solution.py:288
  10.3 12.0 %collective-permute-start.3 = (bf16[512,256]{1,0:T(8,128)(2,1)S(1)}, bf16[512,256]{1,0:T(8,128)(2,1)S(1)}, u32[]{:S(2)}, u32[]{:S(2)}) collective-permute-start(bf16[512,256]{1,0:T(8,128)(2,1)S(1)} %pad_maximum_fusion.3), channel_id=1, source_target_pairs={{0,2},{1,3},{2,0},{3,1},{4,6},{5,7},{6,4},{7,5},{8,10},{9,11},{10,... | collective-permute-start | bytes 786440 | tf_op jit(solution)/shard_map/ppermute | solution.py:285
  11.0 14.0 %collective-permute-start.6 = (bf16[512,256]{1,0:T(8,128)(2,1)}, bf16[512,256]{1,0:T(8,128)(2,1)S(1)}, u32[]{:S(2)}, u32[]{:S(2)}) collective-permute-start(bf16[512,256]{1,0:T(8,128)(2,1)} %pad_maximum_fusion.4), channel_id=1, source_target_pairs={{0,2},{1,3},{2,0},{3,1},{4,6},{5,7},{6,4},{7,5},{8,10},{9,11},{10,... | collective-permute-start | bytes 786440 | tf_op jit(solution)/shard_map/ppermute | solution.py:285
  16.3 11.8 %copy-start.2 = (f32[8192]{0:T(1024)S(1)}, f32[8192]{0:T(1024)}, u32[]{:S(2)}) copy-start(f32[8192]{0:T(1024)} %param.9) | copy-start | bytes 98308
  16.6 11.6 %copy-start.1 = (bf16[512,2048]{1,0:T(8,128)(2,1)S(1)}, bf16[512,2048]{1,0:T(8,128)(2,1)}, u32[]{:S(2)}) copy-start(bf16[512,2048]{1,0:T(8,128)(2,1)} %hid.1) | copy-start | bytes 6291460
  17.8 16.2 %collective-permute-start.4 = (bf16[512,256]{1,0:T(8,128)(2,1)S(1)}, bf16[512,256]{1,0:T(8,128)(2,1)S(1)}, u32[]{:S(2)}, u32[]{:S(2)}) collective-permute-start(bf16[512,256]{1,0:T(8,128)(2,1)S(1)} %broadcast_select_fusion.a0), channel_id=1, source_target_pairs={{0,4},{4,0},{8,12},{12,8},{16,20},{20,16},{24,28},{28,24},{1,5},{5... | collective-permute-start | bytes 786440 | tf_op jit(solution)/shard_map/ppermute | solution.py:308
  19.4 14.7 %collective-permute-start.5 = (bf16[512,256]{1,0:T(8,128)(2,1)S(1)}, bf16[512,256]{1,0:T(8,128)(2,1)S(1)}, u32[]{:S(2)}, u32[]{:S(2)}) collective-permute-start(bf16[512,256]{1,0:T(8,128)(2,1)S(1)} %broadcast_select_fusion.a0), channel_id=1, source_target_pairs={{0,8},{4,12},{8,0},{12,4},{16,24},{20,28},{24,16},{28,20},{1,9},{5... | collective-permute-start | bytes 786440 | tf_op jit(solution)/shard_map/ppermute | solution.py:308
  22.3 12.3 %collective-permute-start.9 = (bf16[512,256]{1,0:T(8,128)(2,1)S(1)}, bf16[512,256]{1,0:T(8,128)(2,1)S(1)}, u32[]{:S(2)}, u32[]{:S(2)}) collective-permute-start(bf16[512,256]{1,0:T(8,128)(2,1)S(1)} %pad_maximum_fusion.5), channel_id=1, source_target_pairs={{0,2},{1,3},{2,0},{3,1},{4,6},{5,7},{6,4},{7,5},{8,10},{9,11},{10,... | collective-permute-start | bytes 786440 | tf_op jit(solution)/shard_map/ppermute | solution.py:285
  25.1 9.6 %collective-permute-start.7 = (bf16[512,256]{1,0:T(8,128)(2,1)S(1)}, bf16[512,256]{1,0:T(8,128)(2,1)S(1)}, u32[]{:S(2)}, u32[]{:S(2)}) collective-permute-start(bf16[512,256]{1,0:T(8,128)(2,1)S(1)} %collective-permute-done.3.b0), channel_id=1, source_target_pairs={{0,4},{4,0},{8,12},{12,8},{16,20},{20,16},{24,28},{28,24},{1,5},{5... | collective-permute-start | bytes 786440 | tf_op jit(solution)/shard_map/ppermute | solution.py:308
  26.6 8.8 %collective-permute-start.8 = (bf16[512,256]{1,0:T(8,128)(2,1)S(1)}, bf16[512,256]{1,0:T(8,128)(2,1)S(1)}, u32[]{:S(2)}, u32[]{:S(2)}) collective-permute-start(bf16[512,256]{1,0:T(8,128)(2,1)S(1)} %collective-permute-done.3.b0), channel_id=1, source_target_pairs={{0,8},{4,12},{8,0},{12,4},{16,24},{20,28},{24,16},{28,20},{1,9},{5... | collective-permute-start | bytes 786440 | tf_op jit(solution)/shard_map/ppermute | solution.py:308
  34.6 7.8 %copy-start = (bf16[64,1024]{1,0:T(8,128)(2,1)S(1)}, bf16[64,1024]{1,0:T(8,128)(2,1)}, u32[]{:S(2)}) copy-start(bf16[64,1024]{1,0:T(8,128)(2,1)} %refs_6_.1) | copy-start | bytes 393220
  36.0 6.5 %collective-permute-start.10 = (bf16[512,128]{1,0:T(8,128)(2,1)S(1)}, bf16[512,128]{1,0:T(8,128)(2,1)S(1)}, u32[]{:S(2)}, u32[]{:S(2)}) collective-permute-start(bf16[512,128]{1,0:T(8,128)(2,1)S(1)} %get-tuple-element.39), channel_id=1, source_target_pairs={{0,2},{1,3},{2,0},{3,1},{4,6},{5,7},{6,4},{7,5},{8,10},{9,11},{10,... | collective-permute-start | bytes 393224 | tf_op jit(solution)/shard_map/ppermute | solution.py:354
  37.0 5.4 %collective-permute-start.11 = (f32[8,128]{1,0:T(8,128)S(1)}, f32[8,128]{1,0:T(8,128)S(1)}, u32[]{:S(2)}, u32[]{:S(2)}) collective-permute-start(f32[8,128]{1,0:T(8,128)S(1)} %get-tuple-element.40.refs_2_), channel_id=1, source_target_pairs={{0,2},{1,3},{2,0},{3,1},{4,6},{5,7},{6,4},{7,5},{8,10},{9,11},{10,... | collective-permute-start | bytes 12296 | tf_op jit(solution)/shard_map/ppermute | solution.py:341
  39.1 9.7 %collective-permute-start.12 = (bf16[512,128]{1,0:T(8,128)(2,1)S(1)}, bf16[512,128]{1,0:T(8,128)(2,1)S(1)}, u32[]{:S(2)}, u32[]{:S(2)}) collective-permute-start(bf16[512,128]{1,0:T(8,128)(2,1)S(1)} %get-tuple-element.44), channel_id=1, source_target_pairs={{0,2},{1,3},{2,0},{3,1},{4,6},{5,7},{6,4},{7,5},{8,10},{9,11},{10,... | collective-permute-start | bytes 393224 | tf_op jit(solution)/shard_map/ppermute | solution.py:355
  44.3 11.2 %all-to-all-start = ((f32[8,2,512]{2,1,0:T(2,128)}), f32[8,2,512]{2,1,0:T(2,128)S(1)}, u32[]{:S(2)}, u32[]{:S(2)}) async-start(f32[8,2,512]{2,1,0:T(2,128)} %get-tuple-element.42.mine), calls=%async_computation | async-start | bytes 65536 | tf_op jit(solution)/shard_map/all_to_all | solution.py:372

commit v2 on v0

--- a/solution.py
+++ b/solution.py
@@ -52,7 +52,7 @@
     return jnp.sum(jnp.where(here, jnp.broadcast_to(row, (n, LANES)), 0.0), axis=1, keepdims=True)
 
 
-def norm_kernel(at, hid, gain, weights, *refs):
+def norm_kernel(at, hid, gain, keys, values, *refs):
     more = refs[:-3]
     normed, sumsq, acc = refs[-3:]
     tok, feats = hid.shape
@@ -71,35 +71,37 @@
                 scale = gain[pl.ds(line + j * (q // LANES) + t, 1), :]
                 normed[rows, lanes] = (raw * scale).astype(BF16)
         sumsq[b : b + 1, :] += to_lanes(jnp.sum(folded, axis=1, keepdims=True))
-    out = more[1][...] if more else None
-    for j in range(GROUP):
-        cols = pl.ds(pl.multiple_of((at[1] ^ j) * q, LANES), q)
-        p = jnp.dot(normed[:, cols], weights[j * q : (j + 1) * q, :], preferred_element_type=F32)
-        out = p if out is None else out + p
-    acc[...] = out
-
-
-def part_of(k, rows, blk):
-    q = blk.shape[0]
-    return jnp.dot(rows[:, k * q : (k + 1) * q], blk[...], preferred_element_type=F32)
-
-
-def early_kernel(mine, other, a0, b0, out):
-    out[...] = part_of(0, mine, a0) + part_of(0, other, b0)
-
-
-def middle_kernel(mine, total, a1, a2, a3, out):
-    acc = total[...]
-    for k, blk in enumerate((a1, a2, a3)):
-        acc = acc + part_of(k + 1, mine, blk)
-    out[...] = acc
-
-
-def late_kernel(other, total, b1, b2, b3, out_k, out_v):
+    blocks = [
+        jnp.concatenate(
+            [w[pl.ds(pl.multiple_of((at[1] ^ k) * q, LANES), q), :] for k in range(GROUP)], axis=0
+        )
+        for w in (keys, values)
+    ]
+    out = jnp.dot(
+        normed[...], jnp.concatenate(blocks, axis=1), preferred_element_type=F32
+    )
+    acc[...] = out + more[1][...] if more else out
+
+
+def part_of(rows, blks):
+    weights = [jnp.concatenate([b[...] for b in blks[side::2]], axis=0) for side in range(2)]
+    return jnp.dot(rows, jnp.concatenate(weights, axis=1), preferred_element_type=F32)
+
+
+def early_kernel(mine, other, a_k, a_v, b_k, b_v, out):
+    q = a_k.shape[0]
+    out[...] = part_of(mine[:, :q], (a_k, a_v)) + part_of(other[:, :q], (b_k, b_v))
+
+
+def middle_kernel(mine, total, *refs):
+    blks, out = refs[:-1], refs[-1]
+    out[...] = total[...] + part_of(mine[:, blks[0].shape[0] :], blks)
+
+
+def late_kernel(other, total, *refs):
+    blks, out_k, out_v = refs[:-2], refs[-2], refs[-1]
     head = out_k.shape[1]
-    acc = total[...]
-    for k, blk in enumerate((b1, b2, b3)):
-        acc = acc + part_of(k + 1, other, blk)
+    acc = total[...] + part_of(other[:, blks[0].shape[0] :], blks)
     out_k[...] = acc[:, :head].astype(BF16)
     out_v[...] = acc[:, head:].astype(BF16)
 
@@ -269,9 +271,7 @@
         return [(j, j ^ bit) for j in range(n_seq)]
 
     def rows_at(start, count):
-        return jnp.concatenate(
-            [lax.dynamic_slice_in_dim(m, start, count) for m in (key_matrix, value_matrix)], axis=1
-        )
+        return [lax.dynamic_slice_in_dim(m, start, count) for m in (key_matrix, value_matrix)]
 
     def crossing(block):
         return [
@@ -284,7 +284,10 @@
 
     def cross(rows):
         return [
-            [lax.ppermute(rows[o - 1][part], "head", shift_x(-o)) for part in range(CORES)]
+            [
+                [lax.ppermute(rows[o - 1][part][side], "head", shift_x(-o)) for side in range(2)]
+                for part in range(CORES)
+            ]
             for o in offsets
         ]
 
@@ -292,14 +295,19 @@
     lead[0][0], key_matrix, value_matrix = lax.optimization_barrier(
         (lead[0][0], key_matrix, value_matrix)
     )
-    firsts = cross([lead[0][:1] + rest[1:] if k == 0 else rest for k, rest in enumerate(crossing(i))])
+    rest = crossing(i)
+    rest[0][0] = lead[0][0]
+    firsts = cross(rest)
     seconds = cross(crossing(3 - i))
     own = [rows_at(start * feats, feats) for start in (h, h ^ 1)]
     swapped = lax.ppermute(hidden, "head", [(j, j ^ 1) for j in range(n_head)])
     blocks = [
         [
             [firsts[o - 1][part]]
-            + [lax.ppermute(firsts[o - 1][part], "seq", flip(bit)) for bit in (1, 2)]
+            + [
+                [lax.ppermute(firsts[o - 1][part][side], "seq", flip(bit)) for side in range(2)]
+                for bit in (1, 2)
+            ]
             + [seconds[o - 1][part]]
             for part in range(CORES)
         ]
@@ -313,9 +321,9 @@
         return call(
             norm_kernel,
             [sds((tok, feats), BF16), sds((lines, LANES), F32), sds((tok, 2 * head), F32)],
-            [SMEM] + [VMEM] * (3 + len(more)),
+            [SMEM] + [VMEM] * (4 + len(more)),
             flops=1 << 30,
-        )(jnp.stack([core * (feats // LANES), i]), rows, gain_lines, own, *more)
+        )(jnp.stack([core * (feats // LANES), i]), rows, gain_lines, *own, *more)
 
     mine, sumsq, acc = norm(h, hidden, own[0], ())
 
@@ -328,7 +336,9 @@
     reach = jnp.broadcast_to((kernel_width - 1) // 2, (1, LANES))
     keep = jnp.broadcast_to(kept_block_count, (1, LANES))
     here = jnp.broadcast_to(s, (1, LANES)).astype(jnp.int32)
-    swapped, room, used, reach = lax.optimization_barrier((swapped, room, used, reach))
+    swapped, room, used, reach, keep, here = lax.optimization_barrier(
+        (swapped, room, used, reach, keep, here)
+    )
     other, sumsq, acc = norm(h ^ 1, swapped, own[1], (sumsq, acc))
     sqs = [sumsq] + [lax.ppermute(sumsq, "head", shift_x(o)) for o in offsets]
 
@@ -336,13 +346,15 @@
     wide, thin = sds((tok, 2 * head), F32), sds((tok, head), BF16)
     for o in offsets:
         half_0, half_1 = blocks[o - 1]
-        part = call(early_kernel, wide, [VMEM] * 4, flops=1 << 29)(
-            mine, other, half_0[0], half_1[0]
+        part = call(early_kernel, wide, [VMEM] * 6, flops=1 << 29)(
+            mine, other, *half_0[0], *half_1[0]
         )
-        part = call(middle_kernel, wide, [VMEM] * 5, flops=1 << 29)(mine, part, *half_0[1:])
+        part = call(middle_kernel, wide, [VMEM] * 8, flops=1 << 29)(
+            mine, part, *sum(half_0[1:], [])
+        )
         part_k, part_v = call(
-            late_kernel, [thin, thin], [VMEM] * 5, flops=1 << 29
-        )(other, part, *half_1[1:])
+            late_kernel, [thin, thin], [VMEM] * 8, flops=1 << 29
+        )(other, part, *sum(half_1[1:], []))
         parts_k.append(lax.ppermute(part_k, "head", shift_x(o)))
         parts_v.append(lax.ppermute(part_v, "head", shift_x(o)))
 

time: 67.3 us -> 72.5 us (1.077)
  blocking collectives: 0 us -> 8.86 us
  waiting for transfers between devices: 17.9 us -> 9.91 us
  starting transfers between devices: 24.8 us -> 29.5 us
  local copies, waits for them, and re-layouts: 6.4 us -> 8.54 us
  other arithmetic: 3.09 us -> 1.3 us
    all_to_all x0 -> x1, blocking collectives: none -> 8.86 us  [local(): said = lax.all_to_all(spread, 'seq', 0, 0, tiled=True)]
    ppermute x8 -> x16, starting transfers between devices: 13.5 us -> 22.2 us  [the longest x8 11.8 us: local(): lax.ppermute(firsts[o - 1][part][side], 'seq', flip(bit))]
    all_to_all x1 -> x0, waiting for transfers between devices: 5.78 us -> none  [local(): said = lax.all_to_all(spread, 'seq', 0, 0, tiled=True)]
    dynamic_slice x5, local copies, waits for them, and re-layouts: 3.32 us -> 6.93 us  [rows_at(): lax.dynamic_slice_in_dim(m, start, count)]
    all_to_all x1 -> x0, starting transfers between devices: 3.25 us -> none  [local(): said = lax.all_to_all(spread, 'seq', 0, 0, tiled=True)]
    ppermute x8 -> x16, waiting for transfers between devices: 4.17 us -> 2.01 us  [the longest x8 1.99 us: cross(): lax.ppermute(rows[o - 1][part][side], 'head', shift_x(-o))]
    concatenate x6 -> x0, other arithmetic: 1.79 us -> none  [rows_at(): jnp.concatenate([lax.dynamic_slice_in_dim(m, start, count) for m in (key_...]
    unnamed x10 -> x6, local copies, waits for them, and re-layouts: 3.07 us -> 1.6 us
  transfers between devices with their start and end apart: 14 -> 21, of which waited for: 5 -> 5; matrix products, arithmetic and copies ran while one was open for 10% -> 11% of each run, Pallas kernels for 13% -> 12%
where the time goes in v2:
time: 72.5 us; the launch traced here: 72 us
  starting transfers between devices  29.5 us (41%)
  Pallas kernels  11.1 us (15%)
  waiting for transfers between devices  9.91 us (14%)
  blocking collectives  8.86 us (12%)
  local copies, waits for them, and re-layouts  8.54 us (12%)
  between operations  2.78 us (4%)
  other arithmetic  1.3 us (2%)
    ppermute x8, starting transfers between devices, local(): lax.ppermute(firsts[o - 1][part][side], 'seq', flip(bit))  11.8 us
    ppermute x8, starting transfers between devices, cross(): lax.ppermute(rows[o - 1][part][side], 'head', shift_x(-o))  10.4 us
    all_to_all x1, blocking collectives, local(): said = lax.all_to_all(spread, 'seq', 0, 0, tiled=True)  8.86 us
    dynamic_slice x5, local copies, waits for them, and re-layouts, rows_at(): lax.dynamic_slice_in_dim(m, start, count)  6.93 us
    all_to_all x1, waiting for transfers between devices, local(): got = lax.all_to_all(stats, 'seq', 0, 0, tiled=True)  6.52 us
    pallas_call x2, Pallas kernels, norm(): call(norm_kernel, [sds((tok, feats), BF16), sds((lines, LANES), F32), sds...  5.39 us
    all_to_all x1, starting transfers between devices, local(): got = lax.all_to_all(stats, 'seq', 0, 0, tiled=True)  4.07 us
    ppermute x8, waiting for transfers between devices, cross(): lax.ppermute(rows[o - 1][part][side], 'head', shift_x(-o))  1.99 us
  transfers between devices with their start and end apart: 21, of which 5 were waited for; matrix products, arithmetic and copies ran while one was open for 11% of the time, Pallas kernels for 12%

profile of v2, /device:TPU:0, one launch (start us, length us, event | category | flops | bytes accessed | tf_op | source)
XLA Modules:
  0.0 72.0 jit_solution(1169670579761438754)
XLA Ops:
  2.2 2.6 %collective-permute-start.1 = (bf16[512,128]{1,0:T(8,128)(2,1)S(1)}, bf16[512,128]{1,0:T(8,128)(2,1)S(1)}, u32[]{:S(2)}, u32[]{:S(2)}) collective-permute-start(bf16[512,128]{1,0:T(8,128)(2,1)S(1)} %get-tuple-element.35), channel_id=1, source_target_pairs={{0,2},{1,3},{2,0},{3,1},{4,6},{5,7},{6,4},{7,5},{8,10},{9,11},{10,... | collective-permute-start | bytes 393224 | tf_op jit(solution)/shard_map/ppermute | solution.py:288
  4.9 1.7 %constant_dynamic-slice_fusion.1 = (bf16[512,128]{1,0:T(8,128)(2,1)S(1)}, bf16[512,128]{1,0:T(8,128)(2,1)S(1)}, bf16[512,128]{1,0:T(8,128)(2,1)}) fusion(bf16[8192,128]{1,0:T(8,128)(2,1)} %param.10, s32[]{:T(128)S(6)} %select_n.87, s32[]{:T(128)S(6)} %select_n.86, s32[]{:T(128)S(6)} %select_n.85), kind=kLoop, calls=%fused_computation.8 | loop fusion | bytes 786444 | tf_op jit(solution)/shard_map/dynamic_slice | solution.py:274
  6.6 1.9 %collective-permute-start.3 = (bf16[512,128]{1,0:T(8,128)(2,1)}, bf16[512,128]{1,0:T(8,128)(2,1)S(1)}, u32[]{:S(2)}, u32[]{:S(2)}) collective-permute-start(bf16[512,128]{1,0:T(8,128)(2,1)} %get-tuple-element.51), channel_id=1, source_target_pairs={{0,2},{1,3},{2,0},{3,1},{4,6},{5,7},{6,4},{7,5},{8,10},{9,11},{10,... | collective-permute-start | bytes 393224 | tf_op jit(solution)/shard_map/ppermute | solution.py:288
  8.5 1.7 %constant_dynamic-slice_fusion = (bf16[512,128]{1,0:T(8,128)(2,1)S(1)}, bf16[512,128]{1,0:T(8,128)(2,1)S(1)}, bf16[512,128]{1,0:T(8,128)(2,1)}) fusion(bf16[8192,128]{1,0:T(8,128)(2,1)} %param.11, s32[]{:T(128)S(6)} %select_n.87, s32[]{:T(128)S(6)} %select_n.86, s32[]{:T(128)S(6)} %select_n.85), kind=kLoop, calls=%fused_computation.7 | loop fusion | bytes 786444 | tf_op jit(solution)/shard_map/dynamic_slice | solution.py:274
  10.3 1.3 %constant_dynamic-slice_fusion.7 = (bf16[2048,128]{1,0:T(8,128)(2,1)S(1)}, bf16[2048,128]{1,0:T(8,128)(2,1)S(1)}) fusion(bf16[8192,128]{1,0:T(8,128)(2,1)} %param.10, s32[]{:T(128)S(6)} %select_n.84, s32[]{:T(128)S(6)} %select_n.83), kind=kLoop, calls=%fused_computation.14 | loop fusion | bytes 2097160 | tf_op jit(solution)/shard_map/dynamic_slice | solution.py:274
  11.6 1.3 %constant_dynamic-slice_fusion.6 = (bf16[2048,128]{1,0:T(8,128)(2,1)S(1)}, bf16[2048,128]{1,0:T(8,128)(2,1)S(1)}) fusion(bf16[8192,128]{1,0:T(8,128)(2,1)} %param.11, s32[]{:T(128)S(6)} %select_n.84, s32[]{:T(128)S(6)} %select_n.83), kind=kLoop, calls=%fused_computation.13 | loop fusion | bytes 2097160 | tf_op jit(solution)/shard_map/dynamic_slice | solution.py:274
  12.9 2.0 %collective-permute-start.9 = (bf16[512,128]{1,0:T(8,128)(2,1)S(1)}, bf16[512,128]{1,0:T(8,128)(2,1)S(1)}, u32[]{:S(2)}, u32[]{:S(2)}) collective-permute-start(bf16[512,128]{1,0:T(8,128)(2,1)S(1)} %get-tuple-element.50), channel_id=1, source_target_pairs={{0,2},{1,3},{2,0},{3,1},{4,6},{5,7},{6,4},{7,5},{8,10},{9,11},{10,... | collective-permute-start | bytes 393224 | tf_op jit(solution)/shard_map/ppermute | solution.py:288
  15.0 2.0 %collective-permute-start.15 = (bf16[512,128]{1,0:T(8,128)(2,1)S(1)}, bf16[512,128]{1,0:T(8,128)(2,1)S(1)}, u32[]{:S(2)}, u32[]{:S(2)}) collective-permute-start(bf16[512,128]{1,0:T(8,128)(2,1)S(1)} %get-tuple-element.49), channel_id=1, source_target_pairs={{0,2},{1,3},{2,0},{3,1},{4,6},{5,7},{6,4},{7,5},{8,10},{9,11},{10,... | collective-permute-start | bytes 393224 | tf_op jit(solution)/shard_map/ppermute | solution.py:288
  17.6 2.0 %collective-permute-start.5 = (bf16[512,128]{1,0:T(8,128)(2,1)S(1)}, bf16[512,128]{1,0:T(8,128)(2,1)S(1)}, u32[]{:S(2)}, u32[]{:S(2)}) collective-permute-start(bf16[512,128]{1,0:T(8,128)(2,1)S(1)} %collective-permute-done.1.a_k), channel_id=1, source_target_pairs={{0,4},{4,0},{8,12},{12,8},{16,20},{20,16},{24,28},{28,24},{1,5},{5... | collective-permute-start | bytes 393224 | tf_op jit(solution)/shard_map/ppermute | solution.py:308
  20.4 2.1 %collective-permute-start.7 = (bf16[512,128]{1,0:T(8,128)(2,1)S(1)}, bf16[512,128]{1,0:T(8,128)(2,1)S(1)}, u32[]{:S(2)}, u32[]{:S(2)}) collective-permute-start(bf16[512,128]{1,0:T(8,128)(2,1)S(1)} %collective-permute-done.1.a_k), channel_id=1, source_target_pairs={{0,8},{4,12},{8,0},{12,4},{16,24},{20,28},{24,16},{28,20},{1,9},{5... | collective-permute-start | bytes 393224 | tf_op jit(solution)/shard_map/ppermute | solution.py:308
  23.2 2.0 %collective-permute-start.6 = (bf16[512,128]{1,0:T(8,128)(2,1)S(1)}, bf16[512,128]{1,0:T(8,128)(2,1)S(1)}, u32[]{:S(2)}, u32[]{:S(2)}) collective-permute-start(bf16[512,128]{1,0:T(8,128)(2,1)S(1)} %collective-permute-done.2.a_v), channel_id=1, source_target_pairs={{0,4},{4,0},{8,12},{12,8},{16,20},{20,16},{24,28},{28,24},{1,5},{5... | collective-permute-start | bytes 393224 | tf_op jit(solution)/shard_map/ppermute | solution.py:308
  25.2 1.6 %collective-permute-start.8 = (bf16[512,128]{1,0:T(8,128)(2,1)S(1)}, bf16[512,128]{1,0:T(8,128)(2,1)S(1)}, u32[]{:S(2)}, u32[]{:S(2)}) collective-permute-start(bf16[512,128]{1,0:T(8,128)(2,1)S(1)} %collective-permute-done.2.a_v), channel_id=1, source_target_pairs={{0,8},{4,12},{8,0},{12,4},{16,24},{20,28},{24,16},{28,20},{1,9},{5... | collective-permute-start | bytes 393224 | tf_op jit(solution)/shard_map/ppermute | solution.py:308
  26.8 1.6 %copy-done.1 = bf16[512,2048]{1,0:T(8,128)(2,1)S(1)} copy-done((bf16[512,2048]{1,0:T(8,128)(2,1)S(1)}, bf16[512,2048]{1,0:T(8,128)(2,1)}, u32[]{:S(2)}) %copy-start.1) | copy-done | bytes 2097176
  28.4 2.2 %shard_map.98 = (bf16[512,2048]{1,0:T(8,128)(2,1)S(1)}, f32[8,128]{1,0:T(8,128)S(1)}, f32[512,256]{1,0:T(8,128)S(1)}) custom-call(s32[2]{0:T(128)S(1)} %get-tuple-element.60.at, bf16[512,2048]{1,0:T(8,128)(2,1)S(1)} %copy-done.1, f32[64,128]{1,0:T(8,128)S(1)} %bitcast.15, bf16[2048,128]{1,0:T(8,128)(2,1)S(1)} %get-tuple-element.54.keys, ...), custom_call_target="tpu_custom_call" | custom-call | flops 1073741824 | bytes 1048576 | tf_op jit(solution)/shard_map/pallas_call | solution.py:321
  32.6 1.6 %collective-permute-start.16 = (bf16[512,128]{1,0:T(8,128)(2,1)S(1)}, bf16[512,128]{1,0:T(8,128)(2,1)S(1)}, u32[]{:S(2)}, u32[]{:S(2)}) collective-permute-start(bf16[512,128]{1,0:T(8,128)(2,1)S(1)} %get-tuple-element.46), channel_id=1, source_target_pairs={{0,2},{1,3},{2,0},{3,1},{4,6},{5,7},{6,4},{7,5},{8,10},{9,11},{10,... | collective-permute-start | bytes 393224 | tf_op jit(solution)/shard_map/ppermute | solution.py:288
  35.1 1.5 %collective-permute-start.12 = (bf16[512,128]{1,0:T(8,128)(2,1)S(1)}, bf16[512,128]{1,0:T(8,128)(2,1)S(1)}, u32[]{:S(2)}, u32[]{:S(2)}) collective-permute-start(bf16[512,128]{1,0:T(8,128)(2,1)S(1)} %collective-permute-done.4.b_v), channel_id=1, source_target_pairs={{0,4},{4,0},{8,12},{12,8},{16,20},{20,16},{24,28},{28,24},{1,5},{5... | collective-permute-start | bytes 393224 | tf_op jit(solution)/shard_map/ppermute | solution.py:308
  36.6 1.6 %collective-permute-start.14 = (bf16[512,128]{1,0:T(8,128)(2,1)S(1)}, bf16[512,128]{1,0:T(8,128)(2,1)S(1)}, u32[]{:S(2)}, u32[]{:S(2)}) collective-permute-start(bf16[512,128]{1,0:T(8,128)(2,1)S(1)} %collective-permute-done.4.b_v), channel_id=1, source_target_pairs={{0,8},{4,12},{8,0},{12,4},{16,24},{20,28},{24,16},{28,20},{1,9},{5... | collective-permute-start | bytes 393224 | tf_op jit(solution)/shard_map/ppermute | solution.py:308
  38.2 3.2 %shard_map.99 = (bf16[512,2048]{1,0:T(8,128)(2,1)S(1)}, f32[8,128]{1,0:T(8,128)S(1)}, f32[512,256]{1,0:T(8,128)S(1)}) custom-call(s32[2]{0:T(128)S(1)} %get-tuple-element.59.at, bf16[512,2048]{1,0:T(8,128)(2,1)} %collective-permute-done.hid, f32[64,128]{1,0:T(8,128)S(1)} %bitcast.16, bf16[2048,128]{1,0:T(8,128)(2,1)S(1)} %get-tuple-element.55.keys, ...), custom_call_target="tpu_custom_call" | custom-call | flops 1073741824 | bytes 1048576 | tf_op jit(solution)/shard_map/pallas_call | solution.py:321
  44.8 1.6 %collective-permute-start.18 = (f32[8,128]{1,0:T(8,128)S(1)}, f32[8,128]{1,0:T(8,128)S(1)}, u32[]{:S(2)}, u32[]{:S(2)}) collective-permute-start(f32[8,128]{1,0:T(8,128)S(1)} %get-tuple-element.38.refs_2_), channel_id=1, source_target_pairs={{0,2},{1,3},{2,0},{3,1},{4,6},{5,7},{6,4},{7,5},{8,10},{9,11},{10,... | collective-permute-start | bytes 12296 | tf_op jit(solution)/shard_map/ppermute | solution.py:343
  47.1 1.4 %collective-permute-done.18.refs_3_ = f32[8,128]{1,0:T(8,128)S(1)} collective-permute-done((f32[8,128]{1,0:T(8,128)S(1)}, f32[8,128]{1,0:T(8,128)S(1)}, u32[]{:S(2)}, u32[]{:S(2)}) %collective-permute-start.18) | collective-permute-done | bytes 4128 | tf_op jit(solution)/shard_map/ppermute | solution.py:343
  48.4 1.8 %shard_map.103 = (f32[512,512]{1,0:T(8,128)S(1)}, f32[8,2,512]{2,1,0:T(2,128)}) custom-call(f32[512,256]{1,0:T(8,128)S(1)} %get-tuple-element.32.refs_0_, bf16[512,128]{1,0:T(8,128)(2,1)S(1)} %collective-permute-done.17.refs_1_, f32[8,128]{1,0:T(8,128)S(1)} %get-tuple-element.38.refs_2_, f32[8,128]{1,0:T(8,128)S(1)} %collective-permute-done.18.refs_3_, ...), custom_call_target="tpu_custom_call" | custom-call | flops 268435456 | bytes 1048576 | tf_op jit(solution)/shard_map/pallas_call | solution.py:369
  50.2 4.1 %all-to-all-start = ((f32[8,2,512]{2,1,0:T(2,128)}), f32[8,2,512]{2,1,0:T(2,128)S(1)}, u32[]{:S(2)}, u32[]{:S(2)}) async-start(f32[8,2,512]{2,1,0:T(2,128)} %get-tuple-element.40.mine), calls=%async_computation | async-start | bytes 65536 | tf_op jit(solution)/shard_map/all_to_all | solution.py:376
  54.5 6.5 %all-to-all-done.got = f32[8,2,512]{2,1,0:T(2,128)S(1)} async-done(((f32[8,2,512]{2,1,0:T(2,128)}), f32[8,2,512]{2,1,0:T(2,128)S(1)}, u32[]{:S(2)}, u32[]{:S(2)}) %all-to-all-start) | async-done | bytes 32800 | tf_op jit(solution)/shard_map/all_to_all | solution.py:376
  62.2 8.9 %all_to_all.16 = f32[8,1,128]{2,1,0:T(1,128)S(1)} all-to-all(f32[8,1,128]{2,1,0:T(1,128)S(1)} %bitcast.13), channel_id=1, replica_groups=mesh['seq'=8,'head'=4] {'seq'}, dimensions={0} | all-to-all | bytes 8192 | tf_op jit(solution)/shard_map/all_to_all | solution.py:387
  (49 shorter events, 11.2 us)
Async XLA Ops:
  0.6 24.6 %collective-permute-start = (bf16[512,2048]{1,0:T(8,128)(2,1)}, bf16[512,2048]{1,0:T(8,128)(2,1)}, u32[]{:S(2)}, u32[]{:S(2)}) collective-permute-start(bf16[512,2048]{1,0:T(8,128)(2,1)} %hid.1), channel_id=1, source_target_pairs={{0,1},{1,0},{2,3},{3,2},{4,5},{5,4},{6,7},{7,6},{8,9},{9,8},{10,11... | collective-permute-start | bytes 6291464 | tf_op jit(solution)/shard_map/ppermute | solution.py:303
  2.2 10.8 %collective-permute-start.1 = (bf16[512,128]{1,0:T(8,128)(2,1)S(1)}, bf16[512,128]{1,0:T(8,128)(2,1)S(1)}, u32[]{:S(2)}, u32[]{:S(2)}) collective-permute-start(bf16[512,128]{1,0:T(8,128)(2,1)S(1)} %get-tuple-element.35), channel_id=1, source_target_pairs={{0,2},{1,3},{2,0},{3,1},{4,6},{5,7},{6,4},{7,5},{8,10},{9,11},{10,... | collective-permute-start | bytes 393224 | tf_op jit(solution)/shard_map/ppermute | solution.py:288
  4.8 10.1 %collective-permute-start.2 = (bf16[512,128]{1,0:T(8,128)(2,1)S(1)}, bf16[512,128]{1,0:T(8,128)(2,1)S(1)}, u32[]{:S(2)}, u32[]{:S(2)}) collective-permute-start(bf16[512,128]{1,0:T(8,128)(2,1)S(1)} %get-tuple-element.36), channel_id=1, source_target_pairs={{0,2},{1,3},{2,0},{3,1},{4,6},{5,7},{6,4},{7,5},{8,10},{9,11},{10,... | collective-permute-start | bytes 393224 | tf_op jit(solution)/shard_map/ppermute | solution.py:288
  6.6 8.5 %collective-permute-start.3 = (bf16[512,128]{1,0:T(8,128)(2,1)}, bf16[512,128]{1,0:T(8,128)(2,1)S(1)}, u32[]{:S(2)}, u32[]{:S(2)}) collective-permute-start(bf16[512,128]{1,0:T(8,128)(2,1)} %get-tuple-element.51), channel_id=1, source_target_pairs={{0,2},{1,3},{2,0},{3,1},{4,6},{5,7},{6,4},{7,5},{8,10},{9,11},{10,... | collective-permute-start | bytes 393224 | tf_op jit(solution)/shard_map/ppermute | solution.py:288
  10.2 7.3 %collective-permute-start.4 = (bf16[512,128]{1,0:T(8,128)(2,1)}, bf16[512,128]{1,0:T(8,128)(2,1)S(1)}, u32[]{:S(2)}, u32[]{:S(2)}) collective-permute-start(bf16[512,128]{1,0:T(8,128)(2,1)} %get-tuple-element.48), channel_id=1, source_target_pairs={{0,2},{1,3},{2,0},{3,1},{4,6},{5,7},{6,4},{7,5},{8,10},{9,11},{10,... | collective-permute-start | bytes 393224 | tf_op jit(solution)/shard_map/ppermute | solution.py:288
  10.3 16.5 %copy-start.2 = (f32[8192]{0:T(1024)S(1)}, f32[8192]{0:T(1024)}, u32[]{:S(2)}) copy-start(f32[8192]{0:T(1024)} %param.9) | copy-start | bytes 98308
  12.9 7.4 %collective-permute-start.9 = (bf16[512,128]{1,0:T(8,128)(2,1)S(1)}, bf16[512,128]{1,0:T(8,128)(2,1)S(1)}, u32[]{:S(2)}, u32[]{:S(2)}) collective-permute-start(bf16[512,128]{1,0:T(8,128)(2,1)S(1)} %get-tuple-element.50), channel_id=1, source_target_pairs={{0,2},{1,3},{2,0},{3,1},{4,6},{5,7},{6,4},{7,5},{8,10},{9,11},{10,... | collective-permute-start | bytes 393224 | tf_op jit(solution)/shard_map/ppermute | solution.py:288
  14.9 8.3 %collective-permute-start.10 = (bf16[512,128]{1,0:T(8,128)(2,1)S(1)}, bf16[512,128]{1,0:T(8,128)(2,1)S(1)}, u32[]{:S(2)}, u32[]{:S(2)}) collective-permute-start(bf16[512,128]{1,0:T(8,128)(2,1)S(1)} %get-tuple-element.47), channel_id=1, source_target_pairs={{0,2},{1,3},{2,0},{3,1},{4,6},{5,7},{6,4},{7,5},{8,10},{9,11},{10,... | collective-permute-start | bytes 393224 | tf_op jit(solution)/shard_map/ppermute | solution.py:288
  15.0 17.5 %collective-permute-start.15 = (bf16[512,128]{1,0:T(8,128)(2,1)S(1)}, bf16[512,128]{1,0:T(8,128)(2,1)S(1)}, u32[]{:S(2)}, u32[]{:S(2)}) collective-permute-start(bf16[512,128]{1,0:T(8,128)(2,1)S(1)} %get-tuple-element.49), channel_id=1, source_target_pairs={{0,2},{1,3},{2,0},{3,1},{4,6},{5,7},{6,4},{7,5},{8,10},{9,11},{10,... | collective-permute-start | bytes 393224 | tf_op jit(solution)/shard_map/ppermute | solution.py:288
  17.6 16.6 %collective-permute-start.5 = (bf16[512,128]{1,0:T(8,128)(2,1)S(1)}, bf16[512,128]{1,0:T(8,128)(2,1)S(1)}, u32[]{:S(2)}, u32[]{:S(2)}) collective-permute-start(bf16[512,128]{1,0:T(8,128)(2,1)S(1)} %collective-permute-done.1.a_k), channel_id=1, source_target_pairs={{0,4},{4,0},{8,12},{12,8},{16,20},{20,16},{24,28},{28,24},{1,5},{5... | collective-permute-start | bytes 393224 | tf_op jit(solution)/shard_map/ppermute | solution.py:308
  20.4 14.8 %collective-permute-start.7 = (bf16[512,128]{1,0:T(8,128)(2,1)S(1)}, bf16[512,128]{1,0:T(8,128)(2,1)S(1)}, u32[]{:S(2)}, u32[]{:S(2)}) collective-permute-start(bf16[512,128]{1,0:T(8,128)(2,1)S(1)} %collective-permute-done.1.a_k), channel_id=1, source_target_pairs={{0,8},{4,12},{8,0},{12,4},{16,24},{20,28},{24,16},{28,20},{1,9},{5... | collective-permute-start | bytes 393224 | tf_op jit(solution)/shard_map/ppermute | solution.py:308
  23.2 11.5 %collective-permute-start.6 = (bf16[512,128]{1,0:T(8,128)(2,1)S(1)}, bf16[512,128]{1,0:T(8,128)(2,1)S(1)}, u32[]{:S(2)}, u32[]{:S(2)}) collective-permute-start(bf16[512,128]{1,0:T(8,128)(2,1)S(1)} %collective-permute-done.2.a_v), channel_id=1, source_target_pairs={{0,4},{4,0},{8,12},{12,8},{16,20},{20,16},{24,28},{28,24},{1,5},{5... | collective-permute-start | bytes 393224 | tf_op jit(solution)/shard_map/ppermute | solution.py:308
  25.2 11.4 %collective-permute-start.8 = (bf16[512,128]{1,0:T(8,128)(2,1)S(1)}, bf16[512,128]{1,0:T(8,128)(2,1)S(1)}, u32[]{:S(2)}, u32[]{:S(2)}) collective-permute-start(bf16[512,128]{1,0:T(8,128)(2,1)S(1)} %collective-permute-done.2.a_v), channel_id=1, source_target_pairs={{0,8},{4,12},{8,0},{12,4},{16,24},{20,28},{24,16},{28,20},{1,9},{5... | collective-permute-start | bytes 393224 | tf_op jit(solution)/shard_map/ppermute | solution.py:308
  26.8 1.6 %copy-start.1 = (bf16[512,2048]{1,0:T(8,128)(2,1)S(1)}, bf16[512,2048]{1,0:T(8,128)(2,1)}, u32[]{:S(2)}) copy-start(bf16[512,2048]{1,0:T(8,128)(2,1)} %hid.1) | copy-start | bytes 6291460
  32.6 9.9 %collective-permute-start.16 = (bf16[512,128]{1,0:T(8,128)(2,1)S(1)}, bf16[512,128]{1,0:T(8,128)(2,1)S(1)}, u32[]{:S(2)}, u32[]{:S(2)}) collective-permute-start(bf16[512,128]{1,0:T(8,128)(2,1)S(1)} %get-tuple-element.46), channel_id=1, source_target_pairs={{0,2},{1,3},{2,0},{3,1},{4,6},{5,7},{6,4},{7,5},{8,10},{9,11},{10,... | collective-permute-start | bytes 393224 | tf_op jit(solution)/shard_map/ppermute | solution.py:288
  34.1 8.4 %collective-permute-start.11 = (bf16[512,128]{1,0:T(8,128)(2,1)S(1)}, bf16[512,128]{1,0:T(8,128)(2,1)S(1)}, u32[]{:S(2)}, u32[]{:S(2)}) collective-permute-start(bf16[512,128]{1,0:T(8,128)(2,1)S(1)} %collective-permute-done.3.b_k), channel_id=1, source_target_pairs={{0,4},{4,0},{8,12},{12,8},{16,20},{20,16},{24,28},{28,24},{1,5},{5... | collective-permute-start | bytes 393224 | tf_op jit(solution)/shard_map/ppermute | solution.py:308
  34.7 7.9 %collective-permute-start.13 = (bf16[512,128]{1,0:T(8,128)(2,1)S(1)}, bf16[512,128]{1,0:T(8,128)(2,1)S(1)}, u32[]{:S(2)}, u32[]{:S(2)}) collective-permute-start(bf16[512,128]{1,0:T(8,128)(2,1)S(1)} %collective-permute-done.3.b_k), channel_id=1, source_target_pairs={{0,8},{4,12},{8,0},{12,4},{16,24},{20,28},{24,16},{28,20},{1,9},{5... | collective-permute-start | bytes 393224 | tf_op jit(solution)/shard_map/ppermute | solution.py:308
  35.1 7.4 %collective-permute-start.12 = (bf16[512,128]{1,0:T(8,128)(2,1)S(1)}, bf16[512,128]{1,0:T(8,128)(2,1)S(1)}, u32[]{:S(2)}, u32[]{:S(2)}) collective-permute-start(bf16[512,128]{1,0:T(8,128)(2,1)S(1)} %collective-permute-done.4.b_v), channel_id=1, source_target_pairs={{0,4},{4,0},{8,12},{12,8},{16,20},{20,16},{24,28},{28,24},{1,5},{5... | collective-permute-start | bytes 393224 | tf_op jit(solution)/shard_map/ppermute | solution.py:308
  36.6 5.9 %collective-permute-start.14 = (bf16[512,128]{1,0:T(8,128)(2,1)S(1)}, bf16[512,128]{1,0:T(8,128)(2,1)S(1)}, u32[]{:S(2)}, u32[]{:S(2)}) collective-permute-start(bf16[512,128]{1,0:T(8,128)(2,1)S(1)} %collective-permute-done.4.b_v), channel_id=1, source_target_pairs={{0,8},{4,12},{8,0},{12,4},{16,24},{20,28},{24,16},{28,20},{1,9},{5... | collective-permute-start | bytes 393224 | tf_op jit(solution)/shard_map/ppermute | solution.py:308
  42.5 5.9 %copy-start = (bf16[64,1024]{1,0:T(8,128)(2,1)S(1)}, bf16[64,1024]{1,0:T(8,128)(2,1)}, u32[]{:S(2)}) copy-start(bf16[64,1024]{1,0:T(8,128)(2,1)} %refs_6_.1) | copy-start | bytes 393220
  43.2 5.3 %collective-permute-start.17 = (bf16[512,128]{1,0:T(8,128)(2,1)S(1)}, bf16[512,128]{1,0:T(8,128)(2,1)S(1)}, u32[]{:S(2)}, u32[]{:S(2)}) collective-permute-start(bf16[512,128]{1,0:T(8,128)(2,1)S(1)} %get-tuple-element.37), channel_id=1, source_target_pairs={{0,2},{1,3},{2,0},{3,1},{4,6},{5,7},{6,4},{7,5},{8,10},{9,11},{10,... | collective-permute-start | bytes 393224 | tf_op jit(solution)/shard_map/ppermute | solution.py:358
  44.8 3.7 %collective-permute-start.18 = (f32[8,128]{1,0:T(8,128)S(1)}, f32[8,128]{1,0:T(8,128)S(1)}, u32[]{:S(2)}, u32[]{:S(2)}) collective-permute-start(f32[8,128]{1,0:T(8,128)S(1)} %get-tuple-element.38.refs_2_), channel_id=1, source_target_pairs={{0,2},{1,3},{2,0},{3,1},{4,6},{5,7},{6,4},{7,5},{8,10},{9,11},{10,... | collective-permute-start | bytes 12296 | tf_op jit(solution)/shard_map/ppermute | solution.py:343
  46.3 8.0 %collective-permute-start.19 = (bf16[512,128]{1,0:T(8,128)(2,1)S(1)}, bf16[512,128]{1,0:T(8,128)(2,1)S(1)}, u32[]{:S(2)}, u32[]{:S(2)}) collective-permute-start(bf16[512,128]{1,0:T(8,128)(2,1)S(1)} %get-tuple-element.42), channel_id=1, source_target_pairs={{0,2},{1,3},{2,0},{3,1},{4,6},{5,7},{6,4},{7,5},{8,10},{9,11},{10,... | collective-permute-start | bytes 393224 | tf_op jit(solution)/shard_map/ppermute | solution.py:359
  50.2 10.8 %all-to-all-start = ((f32[8,2,512]{2,1,0:T(2,128)}), f32[8,2,512]{2,1,0:T(2,128)S(1)}, u32[]{:S(2)}, u32[]{:S(2)}) async-start(f32[8,2,512]{2,1,0:T(2,128)} %get-tuple-element.40.mine), calls=%async_computation | async-start | bytes 65536 | tf_op jit(solution)/shard_map/all_to_all | solution.py:376

commit v3 on v0

--- a/solution.py
+++ b/solution.py
@@ -52,36 +52,30 @@
     return jnp.sum(jnp.where(here, jnp.broadcast_to(row, (n, LANES)), 0.0), axis=1, keepdims=True)
 
 
-def norm_kernel(at, hid, gain, weights, *refs):
+def norm_kernel(flip, hid, gain, weights, *refs):
     more = refs[:-3]
     normed, sumsq, acc = refs[-3:]
     tok, feats = hid.shape
-    q = feats // GROUP
-    line = at[0]
+    line = (lax.axis_index("head") ^ flip) * (feats // LANES)
     sumsq[...] = more[0][...] if more else jnp.zeros_like(sumsq)
     for b in range(tok // LANES):
         rows = pl.ds(b * LANES, LANES)
         folded = None
-        for j in range(GROUP):
-            place = (at[1] ^ j) * q
-            for t in range(q // LANES):
-                raw = hid[rows, pl.ds(j * q + t * LANES, LANES)].astype(F32)
-                folded = raw * raw if folded is None else folded + raw * raw
-                lanes = pl.ds(pl.multiple_of(place + t * LANES, LANES), LANES)
-                scale = gain[pl.ds(line + j * (q // LANES) + t, 1), :]
-                normed[rows, lanes] = (raw * scale).astype(BF16)
+        for t in range(feats // LANES):
+            lanes = pl.ds(t * LANES, LANES)
+            raw = hid[rows, lanes].astype(F32)
+            folded = raw * raw if folded is None else folded + raw * raw
+            normed[rows, lanes] = (raw * gain[pl.ds(line + t, 1), :]).astype(BF16)
         sumsq[b : b + 1, :] += to_lanes(jnp.sum(folded, axis=1, keepdims=True))
-    out = more[1][...] if more else None
-    for j in range(GROUP):
-        cols = pl.ds(pl.multiple_of((at[1] ^ j) * q, LANES), q)
-        p = jnp.dot(normed[:, cols], weights[j * q : (j + 1) * q, :], preferred_element_type=F32)
-        out = p if out is None else out + p
-    acc[...] = out
+    out = jnp.dot(normed[...], weights[...], preferred_element_type=F32)
+    acc[...] = out + more[1][...] if more else out
 
 
 def part_of(k, rows, blk):
     q = blk.shape[0]
-    return jnp.dot(rows[:, k * q : (k + 1) * q], blk[...], preferred_element_type=F32)
+    at = (lax.axis_index("seq") % GROUP) ^ k
+    cols = pl.ds(pl.multiple_of(at * q, LANES), q)
+    return jnp.dot(rows[:, cols], blk[...], preferred_element_type=F32)
 
 
 def early_kernel(mine, other, a0, b0, out):
@@ -268,32 +262,34 @@
     def flip(bit):
         return [(j, j ^ bit) for j in range(n_seq)]
 
+    def sides_at(start, count):
+        return [lax.dynamic_slice_in_dim(m, start, count) for m in (key_matrix, value_matrix)]
+
     def rows_at(start, count):
-        return jnp.concatenate(
-            [lax.dynamic_slice_in_dim(m, start, count) for m in (key_matrix, value_matrix)], axis=1
-        )
-
-    def crossing(block):
-        return [
-            [
-                rows_at(((x - o) % n_x * CORES + (c ^ part)) * feats + block * q, q)
-                for part in range(CORES)
-            ]
-            for o in offsets
+        return jnp.concatenate(sides_at(start, count), axis=1)
+
+    def row_of(o, part, block):
+        return ((x - o) % n_x * CORES + (c ^ part)) * feats + block * q
+
+    def cross(o, rows):
+        return lax.ppermute(rows, "head", shift_x(-o))
+
+    lead = sides_at(row_of(1, 0, i), q)
+    lead, key_matrix, value_matrix = lax.optimization_barrier((lead, key_matrix, value_matrix))
+    lead = [lax.ppermute(rows, "head", shift_x(-1)) for rows in lead]
+    firsts = [
+        [
+            jnp.concatenate(lead, axis=1)
+            if (o, part) == (1, 0)
+            else cross(o, rows_at(row_of(o, part, i), q))
+            for part in range(CORES)
         ]
-
-    def cross(rows):
-        return [
-            [lax.ppermute(rows[o - 1][part], "head", shift_x(-o)) for part in range(CORES)]
-            for o in offsets
-        ]
-
-    lead = crossing(i)
-    lead[0][0], key_matrix, value_matrix = lax.optimization_barrier(
-        (lead[0][0], key_matrix, value_matrix)
-    )
-    firsts = cross([lead[0][:1] + rest[1:] if k == 0 else rest for k, rest in enumerate(crossing(i))])
-    seconds = cross(crossing(3 - i))
+        for o in offsets
+    ]
+    seconds = [
+        [cross(o, rows_at(row_of(o, part, 3 - i), q)) for part in range(CORES)]
+        for o in offsets
+    ]
     own = [rows_at(start * feats, feats) for start in (h, h ^ 1)]
     swapped = lax.ppermute(hidden, "head", [(j, j ^ 1) for j in range(n_head)])
     blocks = [
@@ -309,15 +305,15 @@
     lines = -(-(tok // LANES) // 8) * 8
     gain_lines = gain.reshape(full_width // LANES, LANES)
 
-    def norm(core, rows, own, more):
+    def norm(flip, rows, own, more):
         return call(
-            norm_kernel,
+            functools.partial(norm_kernel, flip),
             [sds((tok, feats), BF16), sds((lines, LANES), F32), sds((tok, 2 * head), F32)],
-            [SMEM] + [VMEM] * (3 + len(more)),
+            [VMEM] * (3 + len(more)),
             flops=1 << 30,
-        )(jnp.stack([core * (feats // LANES), i]), rows, gain_lines, own, *more)
-
-    mine, sumsq, acc = norm(h, hidden, own[0], ())
+        )(rows, gain_lines, own, *more)
+
+    mine, sumsq, acc = norm(0, hidden, own[0], ())
 
     window = queries.shape[0]
     group_heads = queries.shape[1] // head
@@ -328,8 +324,10 @@
     reach = jnp.broadcast_to((kernel_width - 1) // 2, (1, LANES))
     keep = jnp.broadcast_to(kept_block_count, (1, LANES))
     here = jnp.broadcast_to(s, (1, LANES)).astype(jnp.int32)
-    swapped, room, used, reach = lax.optimization_barrier((swapped, room, used, reach))
-    other, sumsq, acc = norm(h ^ 1, swapped, own[1], (sumsq, acc))
+    swapped, room, used, reach, keep, here = lax.optimization_barrier(
+        (swapped, room, used, reach, keep, here)
+    )
+    other, sumsq, acc = norm(1, swapped, own[1], (sumsq, acc))
     sqs = [sumsq] + [lax.ppermute(sumsq, "head", shift_x(o)) for o in offsets]
 
     parts_k, parts_v = [], []

time: 67.3 us -> 64.6 us (0.960)
  blocking collectives: 0 us -> 8.86 us
  waiting for transfers between devices: 17.9 us -> 11 us
  Pallas kernels: 11.8 us -> 9.66 us
  starting transfers between devices: 24.8 us -> 22.7 us
  other arithmetic: 3.09 us -> 1.54 us
  local copies, waits for them, and re-layouts: 6.4 us -> 7.29 us
    all_to_all x0 -> x1, blocking collectives: none -> 8.86 us  [local(): said = lax.all_to_all(spread, 'seq', 0, 0, tiled=True)]
    all_to_all x1 -> x0, waiting for transfers between devices: 5.78 us -> none  [local(): said = lax.all_to_all(spread, 'seq', 0, 0, tiled=True)]
    all_to_all x1 -> x0, starting transfers between devices: 3.25 us -> none  [local(): said = lax.all_to_all(spread, 'seq', 0, 0, tiled=True)]
    pallas_call x2, Pallas kernels: 5.44 us -> 3.91 us  [norm(): call(functools.partial(norm_kernel, flip), [sds((tok, feats), BF16), sds(...]
    concatenate x6 -> x5, other arithmetic: 1.79 us -> 0.32 us  [rows_at(): return jnp.concatenate(sides_at(start, count), axis=1)]
    ppermute x4 -> x5, waiting for transfers between devices: 4.15 us -> 3.02 us  [the longest x3 3.01 us: cross(): return lax.ppermute(rows, 'head', shift_x(-o))]
    all_to_all x1, starting transfers between devices: 3.87 us -> 4.88 us  [local(): got = lax.all_to_all(stats, 'seq', 0, 0, tiled=True)]
    concatenate x0 -> x1, local copies, waits for them, and re-layouts: none -> 0.94 us  [local(): jnp.concatenate(lead, axis=1)]
  transfers between devices with their start and end apart: 14 -> 14, of which waited for: 5 -> 4; matrix products, arithmetic and copies ran while one was open for 10% -> 12% of each run, Pallas kernels for 13% -> 11%
where the time goes in v3:
time: 64.6 us; the launch traced here: 64.1 us
  starting transfers between devices  22.7 us (35%)
  waiting for transfers between devices  11 us (17%)
  Pallas kernels  9.66 us (15%)
  blocking collectives  8.86 us (14%)
  local copies, waits for them, and re-layouts  7.29 us (11%)
  between operations  3.02 us (5%)
  other arithmetic  1.54 us (2%)
    all_to_all x1, blocking collectives, local(): said = lax.all_to_all(spread, 'seq', 0, 0, tiled=True)  8.86 us
    ppermute x4, starting transfers between devices, local(): lax.ppermute(firsts[o - 1][part], 'seq', flip(bit))  7.29 us
    all_to_all x1, waiting for transfers between devices, local(): got = lax.all_to_all(stats, 'seq', 0, 0, tiled=True)  6.51 us
    all_to_all x1, starting transfers between devices, local(): got = lax.all_to_all(stats, 'seq', 0, 0, tiled=True)  4.88 us
    dynamic_slice x5, local copies, waits for them, and re-layouts, sides_at(): lax.dynamic_slice_in_dim(m, start, count)  3.96 us
    pallas_call x2, Pallas kernels, norm(): call(functools.partial(norm_kernel, flip), [sds((tok, feats), BF16), sds(...  3.91 us
    ppermute x3, starting transfers between devices, cross(): return lax.ppermute(rows, 'head', shift_x(-o))  3.71 us
    ppermute x3, waiting for transfers between devices, cross(): return lax.ppermute(rows, 'head', shift_x(-o))  3.01 us
  transfers between devices with their start and end apart: 14, of which 4 were waited for; matrix products, arithmetic and copies ran while one was open for 12% of the time, Pallas kernels for 11%

profile of v3, /device:TPU:0, one launch (start us, length us, event | category | flops | bytes accessed | tf_op | source)
XLA Modules:
  0.0 64.1 jit_solution(15641528548158471222)
XLA Ops:
  1.2 1.7 %constant_dynamic-slice_fusion.10 = (bf16[512,128]{1,0:T(8,128)(2,1)S(1)}, bf16[512,128]{1,0:T(8,128)(2,1)}) fusion(bf16[8192,128]{1,0:T(8,128)(2,1)} %param.11, s32[]{:T(128)S(6)} %select_n.82, bf16[8192,128]{1,0:T(8,128)(2,1)} %param.10), kind=kLoop, calls=%fused_computation.24 | loop fusion | bytes 524292 | tf_op jit(solution)/shard_map/dynamic_slice | solution.py:266
  2.9 2.6 %collective-permute-start.1 = (bf16[512,128]{1,0:T(8,128)(2,1)}, bf16[512,128]{1,0:T(8,128)(2,1)}, u32[]{:S(2)}, u32[]{:S(2)}) collective-permute-start(bf16[512,128]{1,0:T(8,128)(2,1)} %get-tuple-element.35), channel_id=1, source_target_pairs={{0,2},{1,3},{2,0},{3,1},{4,6},{5,7},{6,4},{7,5},{8,10},{9,11},{10,... | collective-permute-start | bytes 393224 | tf_op jit(solution)/shard_map/ppermute | solution.py:279
  5.5 1.1 %constant_dynamic-slice_fusion = (bf16[512,128]{1,0:T(8,128)(2,1)S(1)}, bf16[512,128]{1,0:T(8,128)(2,1)S(1)}, bf16[512,128]{1,0:T(8,128)(2,1)S(1)}) fusion(bf16[8192,128]{1,0:T(8,128)(2,1)} %param.11, s32[]{:T(128)S(6)} %select_n.87, s32[]{:T(128)S(6)} %select_n.86, s32[]{:T(128)S(6)} %select_n.85), kind=kLoop, calls=%fused_computation.14 | loop fusion | bytes 786444 | tf_op jit(solution)/shard_map/dynamic_slice | solution.py:266
  6.6 1.1 %constant_dynamic-slice_fusion.1 = (bf16[512,128]{1,0:T(8,128)(2,1)S(1)}, bf16[512,128]{1,0:T(8,128)(2,1)S(1)}, bf16[512,128]{1,0:T(8,128)(2,1)S(1)}) fusion(bf16[8192,128]{1,0:T(8,128)(2,1)} %param.10, s32[]{:T(128)S(6)} %select_n.87, s32[]{:T(128)S(6)} %select_n.86, s32[]{:T(128)S(6)} %select_n.85), kind=kLoop, calls=%fused_computation.15 | loop fusion | bytes 786444 | tf_op jit(solution)/shard_map/dynamic_slice | solution.py:266
  7.7 2.1 %collective-permute-start.3 = (bf16[512,256]{1,0:T(8,128)(2,1)S(1)}, bf16[512,256]{1,0:T(8,128)(2,1)S(1)}, u32[]{:S(2)}, u32[]{:S(2)}) collective-permute-start(bf16[512,256]{1,0:T(8,128)(2,1)S(1)} %pad_maximum_fusion.2), channel_id=1, source_target_pairs={{0,2},{1,3},{2,0},{3,1},{4,6},{5,7},{6,4},{7,5},{8,10},{9,11},{10,... | collective-permute-start | bytes 786440 | tf_op jit(solution)/shard_map/ppermute | solution.py:275
  10.0 1.4 %copy-done.4 = bf16[8192,128]{1,0:T(8,128)(2,1)S(1)} copy-done((bf16[8192,128]{1,0:T(8,128)(2,1)S(1)}, bf16[8192,128]{1,0:T(8,128)(2,1)}, u32[]{:S(2)}) %copy-start.4) | copy-done | bytes 2097176
  14.5 2.1 %collective-permute-start.4 = (bf16[512,256]{1,0:T(8,128)(2,1)S(1)}, bf16[512,256]{1,0:T(8,128)(2,1)S(1)}, u32[]{:S(2)}, u32[]{:S(2)}) collective-permute-start(bf16[512,256]{1,0:T(8,128)(2,1)S(1)} %constant_dynamic-update-slice_fusion.a0), channel_id=1, source_target_pairs={{0,4},{4,0},{8,12},{12,8},{16,20},{20,16},{24,28},{28,24},{1,5},{5... | collective-permute-start | bytes 786440 | tf_op jit(solution)/shard_map/ppermute | solution.py:298
  16.6 1.6 %collective-permute-start.5 = (bf16[512,256]{1,0:T(8,128)(2,1)S(1)}, bf16[512,256]{1,0:T(8,128)(2,1)S(1)}, u32[]{:S(2)}, u32[]{:S(2)}) collective-permute-start(bf16[512,256]{1,0:T(8,128)(2,1)S(1)} %constant_dynamic-update-slice_fusion.a0), channel_id=1, source_target_pairs={{0,8},{4,12},{8,0},{12,4},{16,24},{20,28},{24,16},{28,20},{1,9},{5... | collective-permute-start | bytes 786440 | tf_op jit(solution)/shard_map/ppermute | solution.py:298
  19.5 1.6 %collective-permute-start.9 = (bf16[512,256]{1,0:T(8,128)(2,1)S(1)}, bf16[512,256]{1,0:T(8,128)(2,1)S(1)}, u32[]{:S(2)}, u32[]{:S(2)}) collective-permute-start(bf16[512,256]{1,0:T(8,128)(2,1)S(1)} %pad_maximum_fusion.4), channel_id=1, source_target_pairs={{0,2},{1,3},{2,0},{3,1},{4,6},{5,7},{6,4},{7,5},{8,10},{9,11},{10,... | collective-permute-start | bytes 786440 | tf_op jit(solution)/shard_map/ppermute | solution.py:275
  21.1 3.0 %collective-permute-done.6.a3 = bf16[512,256]{1,0:T(8,128)(2,1)S(1)} collective-permute-done((bf16[512,256]{1,0:T(8,128)(2,1)S(1)}, bf16[512,256]{1,0:T(8,128)(2,1)S(1)}, u32[]{:S(2)}, u32[]{:S(2)}) %collective-permute-start.6) | collective-permute-done | bytes 262176 | tf_op jit(solution)/shard_map/ppermute | solution.py:275
  24.1 2.1 %collective-permute-start.7 = (bf16[512,256]{1,0:T(8,128)(2,1)S(1)}, bf16[512,256]{1,0:T(8,128)(2,1)S(1)}, u32[]{:S(2)}, u32[]{:S(2)}) collective-permute-start(bf16[512,256]{1,0:T(8,128)(2,1)S(1)} %collective-permute-done.3.b0), channel_id=1, source_target_pairs={{0,4},{4,0},{8,12},{12,8},{16,20},{20,16},{24,28},{28,24},{1,5},{5... | collective-permute-start | bytes 786440 | tf_op jit(solution)/shard_map/ppermute | solution.py:298
  26.1 1.6 %collective-permute-start.8 = (bf16[512,256]{1,0:T(8,128)(2,1)S(1)}, bf16[512,256]{1,0:T(8,128)(2,1)S(1)}, u32[]{:S(2)}, u32[]{:S(2)}) collective-permute-start(bf16[512,256]{1,0:T(8,128)(2,1)S(1)} %collective-permute-done.3.b0), channel_id=1, source_target_pairs={{0,8},{4,12},{8,0},{12,4},{16,24},{20,28},{24,16},{28,20},{1,9},{5... | collective-permute-start | bytes 786440 | tf_op jit(solution)/shard_map/ppermute | solution.py:298
  27.7 1.1 %shard_map.98 = (bf16[512,2048]{1,0:T(8,128)(2,1)S(1)}, f32[8,128]{1,0:T(8,128)S(1)}, f32[512,256]{1,0:T(8,128)S(1)}) custom-call(bf16[512,2048]{1,0:T(8,128)(2,1)S(1)} %copy-done.1, f32[64,128]{1,0:T(8,128)S(1)} %bitcast.12, bf16[2048,256]{1,0:T(8,128)(2,1)S(1)} %pad_maximum_fusion.1.weights), custom_call_target="tpu_custom_call" | custom-call | flops 1073741824 | bytes 1048576 | tf_op jit(solution)/shard_map/pallas_call | solution.py:309
  28.9 2.8 %shard_map.99 = (bf16[512,2048]{1,0:T(8,128)(2,1)S(1)}, f32[8,128]{1,0:T(8,128)S(1)}, f32[512,256]{1,0:T(8,128)S(1)}) custom-call(bf16[512,2048]{1,0:T(8,128)(2,1)} %collective-permute-done.hid, f32[64,128]{1,0:T(8,128)S(1)} %bitcast.13, bf16[2048,256]{1,0:T(8,128)(2,1)S(1)} %pad_maximum_fusion.weights, f32[8,128]{1,0:T(8,128)S(1)} %get-tuple-element.30.refs_0_, ...), custom_call_target="tpu_custom_call" | custom-call | flops 1073741824 | bytes 1048576 | tf_op jit(solution)/shard_map/pallas_call | solution.py:309
  33.5 1.6 %collective-permute-start.10 = (bf16[512,128]{1,0:T(8,128)(2,1)S(1)}, bf16[512,128]{1,0:T(8,128)(2,1)S(1)}, u32[]{:S(2)}, u32[]{:S(2)}) collective-permute-start(bf16[512,128]{1,0:T(8,128)(2,1)S(1)} %get-tuple-element.37), channel_id=1, source_target_pairs={{0,2},{1,3},{2,0},{3,1},{4,6},{5,7},{6,4},{7,5},{8,10},{9,11},{10,... | collective-permute-start | bytes 393224 | tf_op jit(solution)/shard_map/ppermute | solution.py:344
  35.0 1.0 %fusion = (f32[512,64]{1,0:T(8,128)S(1)}, f32[512,64]{1,0:T(8,128)S(1)}, f32[512,64]{1,0:T(8,128)S(1)}) fusion(f32[64]{0:T(128)S(1)} %multiply_power_fusion, f32[512]{0:T(512)S(1)} %add_convert_fusion), kind=kLoop, calls=%fused_computation.9 | loop fusion | flops 65536 | bytes 395520 | tf_op jit(solution)/shard_map/neg | solution.py:353
  36.6 1.5 %collective-permute-start.12 = (bf16[512,128]{1,0:T(8,128)(2,1)S(1)}, bf16[512,128]{1,0:T(8,128)(2,1)S(1)}, u32[]{:S(2)}, u32[]{:S(2)}) collective-permute-start(bf16[512,128]{1,0:T(8,128)(2,1)S(1)} %get-tuple-element.42), channel_id=1, source_target_pairs={{0,2},{1,3},{2,0},{3,1},{4,6},{5,7},{6,4},{7,5},{8,10},{9,11},{10,... | collective-permute-start | bytes 393224 | tf_op jit(solution)/shard_map/ppermute | solution.py:345
  38.3 1.4 %collective-permute-done.11.refs_3_ = f32[8,128]{1,0:T(8,128)S(1)} collective-permute-done((f32[8,128]{1,0:T(8,128)S(1)}, f32[8,128]{1,0:T(8,128)S(1)}, u32[]{:S(2)}, u32[]{:S(2)}) %collective-permute-start.11) | collective-permute-done | bytes 4128 | tf_op jit(solution)/shard_map/ppermute | solution.py:331
  39.7 1.8 %shard_map.103 = (f32[512,512]{1,0:T(8,128)S(1)}, f32[8,2,512]{2,1,0:T(2,128)}) custom-call(f32[512,256]{1,0:T(8,128)S(1)} %get-tuple-element.32.refs_0_, bf16[512,128]{1,0:T(8,128)(2,1)S(1)} %collective-permute-done.10.refs_1_, f32[8,128]{1,0:T(8,128)S(1)} %get-tuple-element.38.refs_2_, f32[8,128]{1,0:T(8,128)S(1)} %collective-permute-done.11.refs_3_, ...), custom_call_target="tpu_custom_call" | custom-call | flops 268435456 | bytes 1048576 | tf_op jit(solution)/shard_map/pallas_call | solution.py:355
  41.5 4.9 %all-to-all-start = ((f32[8,2,512]{2,1,0:T(2,128)}), f32[8,2,512]{2,1,0:T(2,128)S(1)}, u32[]{:S(2)}, u32[]{:S(2)}) async-start(f32[8,2,512]{2,1,0:T(2,128)} %get-tuple-element.40.mine), calls=%async_computation | async-start | bytes 65536 | tf_op jit(solution)/shard_map/all_to_all | solution.py:362
  46.6 6.5 %all-to-all-done.got = f32[8,2,512]{2,1,0:T(2,128)S(1)} async-done(((f32[8,2,512]{2,1,0:T(2,128)}), f32[8,2,512]{2,1,0:T(2,128)S(1)}, u32[]{:S(2)}, u32[]{:S(2)}) %all-to-all-start) | async-done | bytes 32800 | tf_op jit(solution)/shard_map/all_to_all | solution.py:362
  53.1 1.2 %shard_map.105 = f32[8,128]{1,0:T(8,128)S(1)} custom-call(s32[1,128]{1,0:T(1,128)S(1)} %broadcast_in_dim.6.reach, f32[8,2,512]{2,1,0:T(2,128)S(1)} %all-to-all-done.got, f32[8,2,512]{2,1,0:T(2,128)} %get-tuple-element.40.mine, f32[512,512]{1,0:T(8,128)S(1)} %get-tuple-element.41.expo, f32[8,128]{1,0:T(8,128)S(1)} %shard_map.104.vmag, ...), custom_call_target="tpu_custom_call" | custom-call | flops 67108864 | bytes 1048576 | tf_op jit(solution)/shard_map/pallas_call | solution.py:370
  54.3 8.9 %all_to_all.16 = f32[8,1,128]{2,1,0:T(1,128)S(1)} all-to-all(f32[8,1,128]{2,1,0:T(1,128)S(1)} %bitcast.10), channel_id=1, replica_groups=mesh['seq'=8,'head'=4] {'seq'}, dimensions={0} | all-to-all | bytes 8192 | tf_op jit(solution)/shard_map/all_to_all | solution.py:373
  63.1 1.0 %shard_map.106 = (f32[1,4]{1,0:T(1,128)}, f32[1,1]{1,0:T(1,128)}) custom-call(s32[1,128]{1,0:T(1,128)S(1)} %broadcast_in_dim.7.keep, s32[1,128]{1,0:T(1,128)S(1)} %broadcast_in_dim.6.reach, s32[1,128]{1,0:T(1,128)S(1)} %broadcast_in_dim.8.here, f32[8,128]{1,0:T(8,128)S(1)} %bitcast.11), custom_call_target="tpu_custom_call" | custom-call | flops 1048576 | bytes 1048576 | tf_op jit(solution)/shard_map/pallas_call | solution.py:374
  (45 shorter events, 5.8 us)
Async XLA Ops:
  0.6 9.3 %copy-start.3 = (bf16[8192,128]{1,0:T(8,128)(2,1)S(1)}, bf16[8192,128]{1,0:T(8,128)(2,1)}, u32[]{:S(2)}) copy-start(bf16[8192,128]{1,0:T(8,128)(2,1)} %param.11) | copy-start | bytes 6291460
  0.6 25.5 %collective-permute-start = (bf16[512,2048]{1,0:T(8,128)(2,1)}, bf16[512,2048]{1,0:T(8,128)(2,1)}, u32[]{:S(2)}, u32[]{:S(2)}) collective-permute-start(bf16[512,2048]{1,0:T(8,128)(2,1)} %hid.1), channel_id=1, source_target_pairs={{0,1},{1,0},{2,3},{3,2},{4,5},{5,4},{6,7},{7,6},{8,9},{9,8},{10,11... | collective-permute-start | bytes 6291464 | tf_op jit(solution)/shard_map/ppermute | solution.py:294
  2.9 9.7 %collective-permute-start.1 = (bf16[512,128]{1,0:T(8,128)(2,1)}, bf16[512,128]{1,0:T(8,128)(2,1)}, u32[]{:S(2)}, u32[]{:S(2)}) collective-permute-start(bf16[512,128]{1,0:T(8,128)(2,1)} %get-tuple-element.35), channel_id=1, source_target_pairs={{0,2},{1,3},{2,0},{3,1},{4,6},{5,7},{6,4},{7,5},{8,10},{9,11},{10,... | collective-permute-start | bytes 393224 | tf_op jit(solution)/shard_map/ppermute | solution.py:279
  5.5 8.1 %collective-permute-start.2 = (bf16[512,128]{1,0:T(8,128)(2,1)S(1)}, bf16[512,128]{1,0:T(8,128)(2,1)}, u32[]{:S(2)}, u32[]{:S(2)}) collective-permute-start(bf16[512,128]{1,0:T(8,128)(2,1)S(1)} %get-tuple-element.36), channel_id=1, source_target_pairs={{0,2},{1,3},{2,0},{3,1},{4,6},{5,7},{6,4},{7,5},{8,10},{9,11},{10,... | collective-permute-start | bytes 393224 | tf_op jit(solution)/shard_map/ppermute | solution.py:279
  7.7 11.8 %collective-permute-start.3 = (bf16[512,256]{1,0:T(8,128)(2,1)S(1)}, bf16[512,256]{1,0:T(8,128)(2,1)S(1)}, u32[]{:S(2)}, u32[]{:S(2)}) collective-permute-start(bf16[512,256]{1,0:T(8,128)(2,1)S(1)} %pad_maximum_fusion.2), channel_id=1, source_target_pairs={{0,2},{1,3},{2,0},{3,1},{4,6},{5,7},{6,4},{7,5},{8,10},{9,11},{10,... | collective-permute-start | bytes 786440 | tf_op jit(solution)/shard_map/ppermute | solution.py:275
  9.8 14.3 %collective-permute-start.6 = (bf16[512,256]{1,0:T(8,128)(2,1)S(1)}, bf16[512,256]{1,0:T(8,128)(2,1)S(1)}, u32[]{:S(2)}, u32[]{:S(2)}) collective-permute-start(bf16[512,256]{1,0:T(8,128)(2,1)S(1)} %pad_maximum_fusion.3), channel_id=1, source_target_pairs={{0,2},{1,3},{2,0},{3,1},{4,6},{5,7},{6,4},{7,5},{8,10},{9,11},{10,... | collective-permute-start | bytes 786440 | tf_op jit(solution)/shard_map/ppermute | solution.py:275
  9.9 1.6 %copy-start.4 = (bf16[8192,128]{1,0:T(8,128)(2,1)S(1)}, bf16[8192,128]{1,0:T(8,128)(2,1)}, u32[]{:S(2)}) copy-start(bf16[8192,128]{1,0:T(8,128)(2,1)} %param.10) | copy-start | bytes 6291460
  11.5 16.2 %copy-start.1 = (bf16[512,2048]{1,0:T(8,128)(2,1)S(1)}, bf16[512,2048]{1,0:T(8,128)(2,1)}, u32[]{:S(2)}) copy-start(bf16[512,2048]{1,0:T(8,128)(2,1)} %hid.1) | copy-start | bytes 6291460
  11.6 16.2 %copy-start.2 = (f32[8192]{0:T(1024)S(1)}, f32[8192]{0:T(1024)}, u32[]{:S(2)}) copy-start(f32[8192]{0:T(1024)} %param.9) | copy-start | bytes 98308
  14.5 17.6 %collective-permute-start.4 = (bf16[512,256]{1,0:T(8,128)(2,1)S(1)}, bf16[512,256]{1,0:T(8,128)(2,1)S(1)}, u32[]{:S(2)}, u32[]{:S(2)}) collective-permute-start(bf16[512,256]{1,0:T(8,128)(2,1)S(1)} %constant_dynamic-update-slice_fusion.a0), channel_id=1, source_target_pairs={{0,4},{4,0},{8,12},{12,8},{16,20},{20,16},{24,28},{28,24},{1,5},{5... | collective-permute-start | bytes 786440 | tf_op jit(solution)/shard_map/ppermute | solution.py:298
  16.6 15.5 %collective-permute-start.5 = (bf16[512,256]{1,0:T(8,128)(2,1)S(1)}, bf16[512,256]{1,0:T(8,128)(2,1)S(1)}, u32[]{:S(2)}, u32[]{:S(2)}) collective-permute-start(bf16[512,256]{1,0:T(8,128)(2,1)S(1)} %constant_dynamic-update-slice_fusion.a0), channel_id=1, source_target_pairs={{0,8},{4,12},{8,0},{12,4},{16,24},{20,28},{24,16},{28,20},{1,9},{5... | collective-permute-start | bytes 786440 | tf_op jit(solution)/shard_map/ppermute | solution.py:298
  19.5 13.2 %collective-permute-start.9 = (bf16[512,256]{1,0:T(8,128)(2,1)S(1)}, bf16[512,256]{1,0:T(8,128)(2,1)S(1)}, u32[]{:S(2)}, u32[]{:S(2)}) collective-permute-start(bf16[512,256]{1,0:T(8,128)(2,1)S(1)} %pad_maximum_fusion.4), channel_id=1, source_target_pairs={{0,2},{1,3},{2,0},{3,1},{4,6},{5,7},{6,4},{7,5},{8,10},{9,11},{10,... | collective-permute-start | bytes 786440 | tf_op jit(solution)/shard_map/ppermute | solution.py:275
  24.1 8.7 %collective-permute-start.7 = (bf16[512,256]{1,0:T(8,128)(2,1)S(1)}, bf16[512,256]{1,0:T(8,128)(2,1)S(1)}, u32[]{:S(2)}, u32[]{:S(2)}) collective-permute-start(bf16[512,256]{1,0:T(8,128)(2,1)S(1)} %collective-permute-done.3.b0), channel_id=1, source_target_pairs={{0,4},{4,0},{8,12},{12,8},{16,20},{20,16},{24,28},{28,24},{1,5},{5... | collective-permute-start | bytes 786440 | tf_op jit(solution)/shard_map/ppermute | solution.py:298
  26.1 6.7 %collective-permute-start.8 = (bf16[512,256]{1,0:T(8,128)(2,1)S(1)}, bf16[512,256]{1,0:T(8,128)(2,1)S(1)}, u32[]{:S(2)}, u32[]{:S(2)}) collective-permute-start(bf16[512,256]{1,0:T(8,128)(2,1)S(1)} %collective-permute-done.3.b0), channel_id=1, source_target_pairs={{0,8},{4,12},{8,0},{12,4},{16,24},{20,28},{24,16},{28,20},{1,9},{5... | collective-permute-start | bytes 786440 | tf_op jit(solution)/shard_map/ppermute | solution.py:298
  32.7 7.0 %copy-start = (bf16[64,1024]{1,0:T(8,128)(2,1)S(1)}, bf16[64,1024]{1,0:T(8,128)(2,1)}, u32[]{:S(2)}) copy-start(bf16[64,1024]{1,0:T(8,128)(2,1)} %refs_6_.1) | copy-start | bytes 393220
  33.5 6.2 %collective-permute-start.10 = (bf16[512,128]{1,0:T(8,128)(2,1)S(1)}, bf16[512,128]{1,0:T(8,128)(2,1)S(1)}, u32[]{:S(2)}, u32[]{:S(2)}) collective-permute-start(bf16[512,128]{1,0:T(8,128)(2,1)S(1)} %get-tuple-element.37), channel_id=1, source_target_pairs={{0,2},{1,3},{2,0},{3,1},{4,6},{5,7},{6,4},{7,5},{8,10},{9,11},{10,... | collective-permute-start | bytes 393224 | tf_op jit(solution)/shard_map/ppermute | solution.py:344
  36.0 3.7 %collective-permute-start.11 = (f32[8,128]{1,0:T(8,128)S(1)}, f32[8,128]{1,0:T(8,128)S(1)}, u32[]{:S(2)}, u32[]{:S(2)}) collective-permute-start(f32[8,128]{1,0:T(8,128)S(1)} %get-tuple-element.38.refs_2_), channel_id=1, source_target_pairs={{0,2},{1,3},{2,0},{3,1},{4,6},{5,7},{6,4},{7,5},{8,10},{9,11},{10,... | collective-permute-start | bytes 12296 | tf_op jit(solution)/shard_map/ppermute | solution.py:331
  36.6 9.8 %collective-permute-start.12 = (bf16[512,128]{1,0:T(8,128)(2,1)S(1)}, bf16[512,128]{1,0:T(8,128)(2,1)S(1)}, u32[]{:S(2)}, u32[]{:S(2)}) collective-permute-start(bf16[512,128]{1,0:T(8,128)(2,1)S(1)} %get-tuple-element.42), channel_id=1, source_target_pairs={{0,2},{1,3},{2,0},{3,1},{4,6},{5,7},{6,4},{7,5},{8,10},{9,11},{10,... | collective-permute-start | bytes 393224 | tf_op jit(solution)/shard_map/ppermute | solution.py:345
  41.5 11.6 %all-to-all-start = ((f32[8,2,512]{2,1,0:T(2,128)}), f32[8,2,512]{2,1,0:T(2,128)S(1)}, u32[]{:S(2)}, u32[]{:S(2)}) async-start(f32[8,2,512]{2,1,0:T(2,128)} %get-tuple-element.40.mine), calls=%async_computation | async-start | bytes 65536 | tf_op jit(solution)/shard_map/all_to_all | solution.py:362

commit v4 on v0

--- a/solution.py
+++ b/solution.py
@@ -52,36 +52,30 @@
     return jnp.sum(jnp.where(here, jnp.broadcast_to(row, (n, LANES)), 0.0), axis=1, keepdims=True)
 
 
-def norm_kernel(at, hid, gain, weights, *refs):
+def norm_kernel(flip, hid, gain, weights, *refs):
     more = refs[:-3]
     normed, sumsq, acc = refs[-3:]
     tok, feats = hid.shape
-    q = feats // GROUP
-    line = at[0]
+    line = (lax.axis_index("head") ^ flip) * (feats // LANES)
     sumsq[...] = more[0][...] if more else jnp.zeros_like(sumsq)
     for b in range(tok // LANES):
         rows = pl.ds(b * LANES, LANES)
         folded = None
-        for j in range(GROUP):
-            place = (at[1] ^ j) * q
-            for t in range(q // LANES):
-                raw = hid[rows, pl.ds(j * q + t * LANES, LANES)].astype(F32)
-                folded = raw * raw if folded is None else folded + raw * raw
-                lanes = pl.ds(pl.multiple_of(place + t * LANES, LANES), LANES)
-                scale = gain[pl.ds(line + j * (q // LANES) + t, 1), :]
-                normed[rows, lanes] = (raw * scale).astype(BF16)
+        for t in range(feats // LANES):
+            lanes = pl.ds(t * LANES, LANES)
+            raw = hid[rows, lanes].astype(F32)
+            folded = raw * raw if folded is None else folded + raw * raw
+            normed[rows, lanes] = (raw * gain[pl.ds(line + t, 1), :]).astype(BF16)
         sumsq[b : b + 1, :] += to_lanes(jnp.sum(folded, axis=1, keepdims=True))
-    out = more[1][...] if more else None
-    for j in range(GROUP):
-        cols = pl.ds(pl.multiple_of((at[1] ^ j) * q, LANES), q)
-        p = jnp.dot(normed[:, cols], weights[j * q : (j + 1) * q, :], preferred_element_type=F32)
-        out = p if out is None else out + p
-    acc[...] = out
+    out = jnp.dot(normed[...], weights[...], preferred_element_type=F32)
+    acc[...] = out + more[1][...] if more else out
 
 
 def part_of(k, rows, blk):
     q = blk.shape[0]
-    return jnp.dot(rows[:, k * q : (k + 1) * q], blk[...], preferred_element_type=F32)
+    at = (lax.axis_index("seq") % GROUP) ^ k
+    cols = pl.ds(pl.multiple_of(at * q, LANES), q)
+    return jnp.dot(rows[:, cols], blk[...], preferred_element_type=F32)
 
 
 def early_kernel(mine, other, a0, b0, out):
@@ -309,15 +303,15 @@
     lines = -(-(tok // LANES) // 8) * 8
     gain_lines = gain.reshape(full_width // LANES, LANES)
 
-    def norm(core, rows, own, more):
+    def norm(flip, rows, own, more):
         return call(
-            norm_kernel,
+            functools.partial(norm_kernel, flip),
             [sds((tok, feats), BF16), sds((lines, LANES), F32), sds((tok, 2 * head), F32)],
-            [SMEM] + [VMEM] * (3 + len(more)),
+            [VMEM] * (3 + len(more)),
             flops=1 << 30,
-        )(jnp.stack([core * (feats // LANES), i]), rows, gain_lines, own, *more)
-
-    mine, sumsq, acc = norm(h, hidden, own[0], ())
+        )(rows, gain_lines, own, *more)
+
+    mine, sumsq, acc = norm(0, hidden, own[0], ())
 
     window = queries.shape[0]
     group_heads = queries.shape[1] // head
@@ -328,8 +322,10 @@
     reach = jnp.broadcast_to((kernel_width - 1) // 2, (1, LANES))
     keep = jnp.broadcast_to(kept_block_count, (1, LANES))
     here = jnp.broadcast_to(s, (1, LANES)).astype(jnp.int32)
-    swapped, room, used, reach = lax.optimization_barrier((swapped, room, used, reach))
-    other, sumsq, acc = norm(h ^ 1, swapped, own[1], (sumsq, acc))
+    swapped, room, used, reach, keep, here = lax.optimization_barrier(
+        (swapped, room, used, reach, keep, here)
+    )
+    other, sumsq, acc = norm(1, swapped, own[1], (sumsq, acc))
     sqs = [sumsq] + [lax.ppermute(sumsq, "head", shift_x(o)) for o in offsets]
 
     parts_k, parts_v = [], []

time: 67.3 us -> 63.8 us (0.948)
  blocking collectives: 0 us -> 8.86 us
  waiting for transfers between devices: 17.9 us -> 11.6 us
  starting transfers between devices: 24.8 us -> 22.4 us
  Pallas kernels: 11.8 us -> 9.65 us
  local copies, waits for them, and re-layouts: 6.4 us -> 4.85 us
    all_to_all x0 -> x1, blocking collectives: none -> 8.86 us  [local(): said = lax.all_to_all(spread, 'seq', 0, 0, tiled=True)]
    all_to_all x1 -> x0, waiting for transfers between devices: 5.78 us -> none  [local(): said = lax.all_to_all(spread, 'seq', 0, 0, tiled=True)]
    all_to_all x1 -> x0, starting transfers between devices: 3.25 us -> none  [local(): said = lax.all_to_all(spread, 'seq', 0, 0, tiled=True)]
    unnamed x10, local copies, waits for them, and re-layouts: 3.07 us -> 1.52 us
    pallas_call x2, Pallas kernels: 5.44 us -> 3.91 us  [norm(): call(functools.partial(norm_kernel, flip), [sds((tok, feats), BF16), sds(...]
    all_to_all x1, starting transfers between devices: 3.87 us -> 4.88 us  [local(): got = lax.all_to_all(stats, 'seq', 0, 0, tiled=True)]
  transfers between devices with their start and end apart: 14 -> 13, of which waited for: 5 -> 4; matrix products, arithmetic and copies ran while one was open for 10% -> 10% of each run, Pallas kernels for 13% -> 11%
where the time goes in v4:
time: 63.8 us; the launch traced here: 63.4 us
  starting transfers between devices  22.4 us (35%)
  waiting for transfers between devices  11.6 us (18%)
  Pallas kernels  9.65 us (15%)
  blocking collectives  8.86 us (14%)
  local copies, waits for them, and re-layouts  4.85 us (8%)
  other arithmetic  2.99 us (5%)
  between operations  2.98 us (5%)
    all_to_all x1, blocking collectives, local(): said = lax.all_to_all(spread, 'seq', 0, 0, tiled=True)  8.86 us
    ppermute x4, starting transfers between devices, local(): lax.ppermute(firsts[o - 1][part], 'seq', flip(bit))  6.79 us
    ppermute x4, starting transfers between devices, cross(): lax.ppermute(rows[o - 1][part], 'head', shift_x(-o))  6.57 us
    all_to_all x1, waiting for transfers between devices, local(): got = lax.all_to_all(stats, 'seq', 0, 0, tiled=True)  6.51 us
    all_to_all x1, starting transfers between devices, local(): got = lax.all_to_all(stats, 'seq', 0, 0, tiled=True)  4.88 us
    pallas_call x2, Pallas kernels, norm(): call(functools.partial(norm_kernel, flip), [sds((tok, feats), BF16), sds(...  3.91 us
    ppermute x4, waiting for transfers between devices, cross(): lax.ppermute(rows[o - 1][part], 'head', shift_x(-o))  3.6 us
    dynamic_slice x5, local copies, waits for them, and re-layouts, rows_at(): lax.dynamic_slice_in_dim(m, start, count)  3.32 us
  transfers between devices with their start and end apart: 13, of which 4 were waited for; matrix products, arithmetic and copies ran while one was open for 10% of the time, Pallas kernels for 11%

profile of v4, /device:TPU:0, one launch (start us, length us, event | category | flops | bytes accessed | tf_op | source)
XLA Modules:
  0.0 63.4 jit_solution(8997708295660966775)
XLA Ops:
  1.2 1.0 %constant_dynamic-slice_fusion.10 = (bf16[512,128]{1,0:T(8,128)(2,1)S(1)}, bf16[512,128]{1,0:T(8,128)(2,1)S(1)}) fusion(bf16[8192,128]{1,0:T(8,128)(2,1)} %param.11, s32[]{:T(128)S(6)} %select_n.82, bf16[8192,128]{1,0:T(8,128)(2,1)} %param.10), kind=kLoop, calls=%fused_computation.23 | loop fusion | bytes 524292 | tf_op jit(solution)/shard_map/dynamic_slice | solution.py:267
  2.3 2.7 %collective-permute-start.1 = (bf16[512,256]{1,0:T(8,128)(2,1)S(1)}, bf16[512,256]{1,0:T(8,128)(2,1)S(1)}, u32[]{:S(2)}, u32[]{:S(2)}) collective-permute-start(bf16[512,256]{1,0:T(8,128)(2,1)S(1)} %pad_maximum_fusion.2), channel_id=1, source_target_pairs={{0,2},{1,3},{2,0},{3,1},{4,6},{5,7},{6,4},{7,5},{8,10},{9,11},{10,... | collective-permute-start | bytes 786440 | tf_op jit(solution)/shard_map/ppermute | solution.py:281
  5.0 1.1 %constant_dynamic-slice_fusion = (bf16[512,128]{1,0:T(8,128)(2,1)S(1)}, bf16[512,128]{1,0:T(8,128)(2,1)S(1)}, bf16[512,128]{1,0:T(8,128)(2,1)S(1)}) fusion(bf16[8192,128]{1,0:T(8,128)(2,1)} %param.11, s32[]{:T(128)S(6)} %select_n.87, s32[]{:T(128)S(6)} %select_n.86, s32[]{:T(128)S(6)} %select_n.85), kind=kLoop, calls=%fused_computation.13 | loop fusion | bytes 786444 | tf_op jit(solution)/shard_map/dynamic_slice | solution.py:267
  6.0 1.1 %constant_dynamic-slice_fusion.1 = (bf16[512,128]{1,0:T(8,128)(2,1)S(1)}, bf16[512,128]{1,0:T(8,128)(2,1)S(1)}, bf16[512,128]{1,0:T(8,128)(2,1)S(1)}) fusion(bf16[8192,128]{1,0:T(8,128)(2,1)} %param.10, s32[]{:T(128)S(6)} %select_n.87, s32[]{:T(128)S(6)} %select_n.86, s32[]{:T(128)S(6)} %select_n.85), kind=kLoop, calls=%fused_computation.14 | loop fusion | bytes 786444 | tf_op jit(solution)/shard_map/dynamic_slice | solution.py:267
  8.6 2.0 %collective-permute-start.5 = (bf16[512,256]{1,0:T(8,128)(2,1)}, bf16[512,256]{1,0:T(8,128)(2,1)S(1)}, u32[]{:S(2)}, u32[]{:S(2)}) collective-permute-start(bf16[512,256]{1,0:T(8,128)(2,1)} %pad_maximum_fusion.4), channel_id=1, source_target_pairs={{0,2},{1,3},{2,0},{3,1},{4,6},{5,7},{6,4},{7,5},{8,10},{9,11},{10,... | collective-permute-start | bytes 786440 | tf_op jit(solution)/shard_map/ppermute | solution.py:281
  10.7 1.5 %copy-done.4 = bf16[8192,128]{1,0:T(8,128)(2,1)S(1)} copy-done((bf16[8192,128]{1,0:T(8,128)(2,1)S(1)}, bf16[8192,128]{1,0:T(8,128)(2,1)}, u32[]{:S(2)}) %copy-start.4) | copy-done | bytes 2097176
  13.4 1.6 %collective-permute-start.3 = (bf16[512,256]{1,0:T(8,128)(2,1)S(1)}, bf16[512,256]{1,0:T(8,128)(2,1)S(1)}, u32[]{:S(2)}, u32[]{:S(2)}) collective-permute-start(bf16[512,256]{1,0:T(8,128)(2,1)S(1)} %collective-permute-done.1.a0), channel_id=1, source_target_pairs={{0,4},{4,0},{8,12},{12,8},{16,20},{20,16},{24,28},{28,24},{1,5},{5... | collective-permute-start | bytes 786440 | tf_op jit(solution)/shard_map/ppermute | solution.py:296
  15.0 1.6 %collective-permute-start.4 = (bf16[512,256]{1,0:T(8,128)(2,1)S(1)}, bf16[512,256]{1,0:T(8,128)(2,1)S(1)}, u32[]{:S(2)}, u32[]{:S(2)}) collective-permute-start(bf16[512,256]{1,0:T(8,128)(2,1)S(1)} %collective-permute-done.1.a0), channel_id=1, source_target_pairs={{0,8},{4,12},{8,0},{12,4},{16,24},{20,28},{24,16},{28,20},{1,9},{5... | collective-permute-start | bytes 786440 | tf_op jit(solution)/shard_map/ppermute | solution.py:296
  17.9 1.9 %collective-permute-start.8 = (bf16[512,256]{1,0:T(8,128)(2,1)S(1)}, bf16[512,256]{1,0:T(8,128)(2,1)S(1)}, u32[]{:S(2)}, u32[]{:S(2)}) collective-permute-start(bf16[512,256]{1,0:T(8,128)(2,1)S(1)} %pad_maximum_fusion.5), channel_id=1, source_target_pairs={{0,2},{1,3},{2,0},{3,1},{4,6},{5,7},{6,4},{7,5},{8,10},{9,11},{10,... | collective-permute-start | bytes 786440 | tf_op jit(solution)/shard_map/ppermute | solution.py:281
  19.8 3.6 %collective-permute-done.5.a3 = bf16[512,256]{1,0:T(8,128)(2,1)S(1)} collective-permute-done((bf16[512,256]{1,0:T(8,128)(2,1)}, bf16[512,256]{1,0:T(8,128)(2,1)S(1)}, u32[]{:S(2)}, u32[]{:S(2)}) %collective-permute-start.5) | collective-permute-done | bytes 262176 | tf_op jit(solution)/shard_map/ppermute | solution.py:281
  23.4 2.0 %collective-permute-start.6 = (bf16[512,256]{1,0:T(8,128)(2,1)S(1)}, bf16[512,256]{1,0:T(8,128)(2,1)S(1)}, u32[]{:S(2)}, u32[]{:S(2)}) collective-permute-start(bf16[512,256]{1,0:T(8,128)(2,1)S(1)} %collective-permute-done.2.b0), channel_id=1, source_target_pairs={{0,4},{4,0},{8,12},{12,8},{16,20},{20,16},{24,28},{28,24},{1,5},{5... | collective-permute-start | bytes 786440 | tf_op jit(solution)/shard_map/ppermute | solution.py:296
  25.4 1.6 %collective-permute-start.7 = (bf16[512,256]{1,0:T(8,128)(2,1)S(1)}, bf16[512,256]{1,0:T(8,128)(2,1)S(1)}, u32[]{:S(2)}, u32[]{:S(2)}) collective-permute-start(bf16[512,256]{1,0:T(8,128)(2,1)S(1)} %collective-permute-done.2.b0), channel_id=1, source_target_pairs={{0,8},{4,12},{8,0},{12,4},{16,24},{20,28},{24,16},{28,20},{1,9},{5... | collective-permute-start | bytes 786440 | tf_op jit(solution)/shard_map/ppermute | solution.py:296
  27.0 1.1 %shard_map.98 = (bf16[512,2048]{1,0:T(8,128)(2,1)S(1)}, f32[8,128]{1,0:T(8,128)S(1)}, f32[512,256]{1,0:T(8,128)S(1)}) custom-call(bf16[512,2048]{1,0:T(8,128)(2,1)S(1)} %copy-done.1, f32[64,128]{1,0:T(8,128)S(1)} %bitcast.12, bf16[2048,256]{1,0:T(8,128)(2,1)S(1)} %pad_maximum_fusion.1.weights), custom_call_target="tpu_custom_call" | custom-call | flops 1073741824 | bytes 1048576 | tf_op jit(solution)/shard_map/pallas_call | solution.py:307
  28.2 2.8 %shard_map.99 = (bf16[512,2048]{1,0:T(8,128)(2,1)S(1)}, f32[8,128]{1,0:T(8,128)S(1)}, f32[512,256]{1,0:T(8,128)S(1)}) custom-call(bf16[512,2048]{1,0:T(8,128)(2,1)} %collective-permute-done.hid, f32[64,128]{1,0:T(8,128)S(1)} %bitcast.13, bf16[2048,256]{1,0:T(8,128)(2,1)S(1)} %pad_maximum_fusion.weights, f32[8,128]{1,0:T(8,128)S(1)} %get-tuple-element.29.refs_0_, ...), custom_call_target="tpu_custom_call" | custom-call | flops 1073741824 | bytes 1048576 | tf_op jit(solution)/shard_map/pallas_call | solution.py:307
  32.7 1.6 %collective-permute-start.9 = (bf16[512,128]{1,0:T(8,128)(2,1)S(1)}, bf16[512,128]{1,0:T(8,128)(2,1)S(1)}, u32[]{:S(2)}, u32[]{:S(2)}) collective-permute-start(bf16[512,128]{1,0:T(8,128)(2,1)S(1)} %get-tuple-element.35), channel_id=1, source_target_pairs={{0,2},{1,3},{2,0},{3,1},{4,6},{5,7},{6,4},{7,5},{8,10},{9,11},{10,... | collective-permute-start | bytes 393224 | tf_op jit(solution)/shard_map/ppermute | solution.py:342
  34.3 1.0 %fusion = (f32[512,64]{1,0:T(8,128)S(1)}, f32[512,64]{1,0:T(8,128)S(1)}, f32[512,64]{1,0:T(8,128)S(1)}) fusion(f32[64]{0:T(128)S(1)} %multiply_power_fusion, f32[512]{0:T(512)S(1)} %add_convert_fusion), kind=kLoop, calls=%fused_computation.10 | loop fusion | flops 65536 | bytes 395520 | tf_op jit(solution)/shard_map/neg | solution.py:351
  35.9 1.5 %collective-permute-start.11 = (bf16[512,128]{1,0:T(8,128)(2,1)S(1)}, bf16[512,128]{1,0:T(8,128)(2,1)S(1)}, u32[]{:S(2)}, u32[]{:S(2)}) collective-permute-start(bf16[512,128]{1,0:T(8,128)(2,1)S(1)} %get-tuple-element.40), channel_id=1, source_target_pairs={{0,2},{1,3},{2,0},{3,1},{4,6},{5,7},{6,4},{7,5},{8,10},{9,11},{10,... | collective-permute-start | bytes 393224 | tf_op jit(solution)/shard_map/ppermute | solution.py:343
  37.6 1.4 %collective-permute-done.10.refs_3_ = f32[8,128]{1,0:T(8,128)S(1)} collective-permute-done((f32[8,128]{1,0:T(8,128)S(1)}, f32[8,128]{1,0:T(8,128)S(1)}, u32[]{:S(2)}, u32[]{:S(2)}) %collective-permute-start.10) | collective-permute-done | bytes 4128 | tf_op jit(solution)/shard_map/ppermute | solution.py:329
  39.0 1.8 %shard_map.103 = (f32[512,512]{1,0:T(8,128)S(1)}, f32[8,2,512]{2,1,0:T(2,128)}) custom-call(f32[512,256]{1,0:T(8,128)S(1)} %get-tuple-element.31.refs_0_, bf16[512,128]{1,0:T(8,128)(2,1)S(1)} %collective-permute-done.9.refs_1_, f32[8,128]{1,0:T(8,128)S(1)} %get-tuple-element.36.refs_2_, f32[8,128]{1,0:T(8,128)S(1)} %collective-permute-done.10.refs_3_, ...), custom_call_target="tpu_custom_call" | custom-call | flops 268435456 | bytes 1048576 | tf_op jit(solution)/shard_map/pallas_call | solution.py:353
  40.8 4.9 %all-to-all-start = ((f32[8,2,512]{2,1,0:T(2,128)}), f32[8,2,512]{2,1,0:T(2,128)S(1)}, u32[]{:S(2)}, u32[]{:S(2)}) async-start(f32[8,2,512]{2,1,0:T(2,128)} %get-tuple-element.38.mine), calls=%async_computation | async-start | bytes 65536 | tf_op jit(solution)/shard_map/all_to_all | solution.py:360
  45.8 6.5 %all-to-all-done.got = f32[8,2,512]{2,1,0:T(2,128)S(1)} async-done(((f32[8,2,512]{2,1,0:T(2,128)}), f32[8,2,512]{2,1,0:T(2,128)S(1)}, u32[]{:S(2)}, u32[]{:S(2)}) %all-to-all-start) | async-done | bytes 32800 | tf_op jit(solution)/shard_map/all_to_all | solution.py:360
  52.3 1.2 %shard_map.105 = f32[8,128]{1,0:T(8,128)S(1)} custom-call(s32[1,128]{1,0:T(1,128)S(1)} %broadcast_in_dim.6.reach, f32[8,2,512]{2,1,0:T(2,128)S(1)} %all-to-all-done.got, f32[8,2,512]{2,1,0:T(2,128)} %get-tuple-element.38.mine, f32[512,512]{1,0:T(8,128)S(1)} %get-tuple-element.39.expo, f32[8,128]{1,0:T(8,128)S(1)} %shard_map.104.vmag, ...), custom_call_target="tpu_custom_call" | custom-call | flops 67108864 | bytes 1048576 | tf_op jit(solution)/shard_map/pallas_call | solution.py:368
  53.5 8.9 %all_to_all.16 = f32[8,1,128]{2,1,0:T(1,128)S(1)} all-to-all(f32[8,1,128]{2,1,0:T(1,128)S(1)} %bitcast.10), channel_id=1, replica_groups=mesh['seq'=8,'head'=4] {'seq'}, dimensions={0} | all-to-all | bytes 8192 | tf_op jit(solution)/shard_map/all_to_all | solution.py:371
  62.4 1.0 %shard_map.106 = (f32[1,4]{1,0:T(1,128)}, f32[1,1]{1,0:T(1,128)}) custom-call(s32[1,128]{1,0:T(1,128)S(1)} %broadcast_in_dim.7.keep, s32[1,128]{1,0:T(1,128)S(1)} %broadcast_in_dim.6.reach, s32[1,128]{1,0:T(1,128)S(1)} %broadcast_in_dim.8.here, f32[8,128]{1,0:T(8,128)S(1)} %bitcast.11), custom_call_target="tpu_custom_call" | custom-call | flops 1048576 | bytes 1048576 | tf_op jit(solution)/shard_map/pallas_call | solution.py:372
  (42 shorter events, 5.3 us)
Async XLA Ops:
  0.6 10.0 %copy-start.3 = (bf16[8192,128]{1,0:T(8,128)(2,1)S(1)}, bf16[8192,128]{1,0:T(8,128)(2,1)}, u32[]{:S(2)}) copy-start(bf16[8192,128]{1,0:T(8,128)(2,1)} %param.11) | copy-start | bytes 6291460
  0.6 24.8 %collective-permute-start = (bf16[512,2048]{1,0:T(8,128)(2,1)}, bf16[512,2048]{1,0:T(8,128)(2,1)}, u32[]{:S(2)}, u32[]{:S(2)}) collective-permute-start(bf16[512,2048]{1,0:T(8,128)(2,1)} %hid.1), channel_id=1, source_target_pairs={{0,1},{1,0},{2,3},{3,2},{4,5},{5,4},{6,7},{7,6},{8,9},{9,8},{10,11... | collective-permute-start | bytes 6291464 | tf_op jit(solution)/shard_map/ppermute | solution.py:292
  2.3 11.1 %collective-permute-start.1 = (bf16[512,256]{1,0:T(8,128)(2,1)S(1)}, bf16[512,256]{1,0:T(8,128)(2,1)S(1)}, u32[]{:S(2)}, u32[]{:S(2)}) collective-permute-start(bf16[512,256]{1,0:T(8,128)(2,1)S(1)} %pad_maximum_fusion.2), channel_id=1, source_target_pairs={{0,2},{1,3},{2,0},{3,1},{4,6},{5,7},{6,4},{7,5},{8,10},{9,11},{10,... | collective-permute-start | bytes 786440 | tf_op jit(solution)/shard_map/ppermute | solution.py:281
  7.8 10.1 %collective-permute-start.2 = (bf16[512,256]{1,0:T(8,128)(2,1)}, bf16[512,256]{1,0:T(8,128)(2,1)S(1)}, u32[]{:S(2)}, u32[]{:S(2)}) collective-permute-start(bf16[512,256]{1,0:T(8,128)(2,1)} %pad_maximum_fusion.3), channel_id=1, source_target_pairs={{0,2},{1,3},{2,0},{3,1},{4,6},{5,7},{6,4},{7,5},{8,10},{9,11},{10,... | collective-permute-start | bytes 786440 | tf_op jit(solution)/shard_map/ppermute | solution.py:281
  8.6 14.7 %collective-permute-start.5 = (bf16[512,256]{1,0:T(8,128)(2,1)}, bf16[512,256]{1,0:T(8,128)(2,1)S(1)}, u32[]{:S(2)}, u32[]{:S(2)}) collective-permute-start(bf16[512,256]{1,0:T(8,128)(2,1)} %pad_maximum_fusion.4), channel_id=1, source_target_pairs={{0,2},{1,3},{2,0},{3,1},{4,6},{5,7},{6,4},{7,5},{8,10},{9,11},{10,... | collective-permute-start | bytes 786440 | tf_op jit(solution)/shard_map/ppermute | solution.py:281
  10.6 1.6 %copy-start.4 = (bf16[8192,128]{1,0:T(8,128)(2,1)S(1)}, bf16[8192,128]{1,0:T(8,128)(2,1)}, u32[]{:S(2)}) copy-start(bf16[8192,128]{1,0:T(8,128)(2,1)} %param.10) | copy-start | bytes 6291460
  12.3 14.7 %copy-start.1 = (bf16[512,2048]{1,0:T(8,128)(2,1)S(1)}, bf16[512,2048]{1,0:T(8,128)(2,1)}, u32[]{:S(2)}) copy-start(bf16[512,2048]{1,0:T(8,128)(2,1)} %hid.1) | copy-start | bytes 6291460
  12.3 14.7 %copy-start.2 = (f32[8192]{0:T(1024)S(1)}, f32[8192]{0:T(1024)}, u32[]{:S(2)}) copy-start(f32[8192]{0:T(1024)} %param.9) | copy-start | bytes 98308
  13.4 18.0 %collective-permute-start.3 = (bf16[512,256]{1,0:T(8,128)(2,1)S(1)}, bf16[512,256]{1,0:T(8,128)(2,1)S(1)}, u32[]{:S(2)}, u32[]{:S(2)}) collective-permute-start(bf16[512,256]{1,0:T(8,128)(2,1)S(1)} %collective-permute-done.1.a0), channel_id=1, source_target_pairs={{0,4},{4,0},{8,12},{12,8},{16,20},{20,16},{24,28},{28,24},{1,5},{5... | collective-permute-start | bytes 786440 | tf_op jit(solution)/shard_map/ppermute | solution.py:296
  15.0 16.4 %collective-permute-start.4 = (bf16[512,256]{1,0:T(8,128)(2,1)S(1)}, bf16[512,256]{1,0:T(8,128)(2,1)S(1)}, u32[]{:S(2)}, u32[]{:S(2)}) collective-permute-start(bf16[512,256]{1,0:T(8,128)(2,1)S(1)} %collective-permute-done.1.a0), channel_id=1, source_target_pairs={{0,8},{4,12},{8,0},{12,4},{16,24},{20,28},{24,16},{28,20},{1,9},{5... | collective-permute-start | bytes 786440 | tf_op jit(solution)/shard_map/ppermute | solution.py:296
  17.9 14.1 %collective-permute-start.8 = (bf16[512,256]{1,0:T(8,128)(2,1)S(1)}, bf16[512,256]{1,0:T(8,128)(2,1)S(1)}, u32[]{:S(2)}, u32[]{:S(2)}) collective-permute-start(bf16[512,256]{1,0:T(8,128)(2,1)S(1)} %pad_maximum_fusion.5), channel_id=1, source_target_pairs={{0,2},{1,3},{2,0},{3,1},{4,6},{5,7},{6,4},{7,5},{8,10},{9,11},{10,... | collective-permute-start | bytes 786440 | tf_op jit(solution)/shard_map/ppermute | solution.py:281
  23.4 8.7 %collective-permute-start.6 = (bf16[512,256]{1,0:T(8,128)(2,1)S(1)}, bf16[512,256]{1,0:T(8,128)(2,1)S(1)}, u32[]{:S(2)}, u32[]{:S(2)}) collective-permute-start(bf16[512,256]{1,0:T(8,128)(2,1)S(1)} %collective-permute-done.2.b0), channel_id=1, source_target_pairs={{0,4},{4,0},{8,12},{12,8},{16,20},{20,16},{24,28},{28,24},{1,5},{5... | collective-permute-start | bytes 786440 | tf_op jit(solution)/shard_map/ppermute | solution.py:296
  25.4 6.7 %collective-permute-start.7 = (bf16[512,256]{1,0:T(8,128)(2,1)S(1)}, bf16[512,256]{1,0:T(8,128)(2,1)S(1)}, u32[]{:S(2)}, u32[]{:S(2)}) collective-permute-start(bf16[512,256]{1,0:T(8,128)(2,1)S(1)} %collective-permute-done.2.b0), channel_id=1, source_target_pairs={{0,8},{4,12},{8,0},{12,4},{16,24},{20,28},{24,16},{28,20},{1,9},{5... | collective-permute-start | bytes 786440 | tf_op jit(solution)/shard_map/ppermute | solution.py:296
  32.0 7.0 %copy-start = (bf16[64,1024]{1,0:T(8,128)(2,1)S(1)}, bf16[64,1024]{1,0:T(8,128)(2,1)}, u32[]{:S(2)}) copy-start(bf16[64,1024]{1,0:T(8,128)(2,1)} %refs_6_.1) | copy-start | bytes 393220
  32.7 6.2 %collective-permute-start.9 = (bf16[512,128]{1,0:T(8,128)(2,1)S(1)}, bf16[512,128]{1,0:T(8,128)(2,1)S(1)}, u32[]{:S(2)}, u32[]{:S(2)}) collective-permute-start(bf16[512,128]{1,0:T(8,128)(2,1)S(1)} %get-tuple-element.35), channel_id=1, source_target_pairs={{0,2},{1,3},{2,0},{3,1},{4,6},{5,7},{6,4},{7,5},{8,10},{9,11},{10,... | collective-permute-start | bytes 393224 | tf_op jit(solution)/shard_map/ppermute | solution.py:342
  35.3 3.7 %collective-permute-start.10 = (f32[8,128]{1,0:T(8,128)S(1)}, f32[8,128]{1,0:T(8,128)S(1)}, u32[]{:S(2)}, u32[]{:S(2)}) collective-permute-start(f32[8,128]{1,0:T(8,128)S(1)} %get-tuple-element.36.refs_2_), channel_id=1, source_target_pairs={{0,2},{1,3},{2,0},{3,1},{4,6},{5,7},{6,4},{7,5},{8,10},{9,11},{10,... | collective-permute-start | bytes 12296 | tf_op jit(solution)/shard_map/ppermute | solution.py:329
  35.9 9.8 %collective-permute-start.11 = (bf16[512,128]{1,0:T(8,128)(2,1)S(1)}, bf16[512,128]{1,0:T(8,128)(2,1)S(1)}, u32[]{:S(2)}, u32[]{:S(2)}) collective-permute-start(bf16[512,128]{1,0:T(8,128)(2,1)S(1)} %get-tuple-element.40), channel_id=1, source_target_pairs={{0,2},{1,3},{2,0},{3,1},{4,6},{5,7},{6,4},{7,5},{8,10},{9,11},{10,... | collective-permute-start | bytes 393224 | tf_op jit(solution)/shard_map/ppermute | solution.py:343
  40.8 11.6 %all-to-all-start = ((f32[8,2,512]{2,1,0:T(2,128)}), f32[8,2,512]{2,1,0:T(2,128)S(1)}, u32[]{:S(2)}, u32[]{:S(2)}) async-start(f32[8,2,512]{2,1,0:T(2,128)} %get-tuple-element.38.mine), calls=%async_computation | async-start | bytes 65536 | tf_op jit(solution)/shard_map/all_to_all | solution.py:360
